TPU v7x, 512 devices: a 8x2x16 block of a 8x16x16 slice. The times are simulated.
512 devices in a mesh: groups: 2 (over y), expert: 32 (over z, core), mp: 8 (over x).
Axes of the slice: x: 8, y: 2, z: 16, core: 2. Of those that a mesh axis runs over, the one named last changes fastest.
The devices are a block of a 8x16x16 slice.
Arguments:
- tokens: bfloat16 [49152, 1024], P(('groups', 'expert'), 'mp'), parts along dimension 0, may hold values from -60 to 60
- gain: float32 [1024], replicated, may hold values from 0.1 to 1.9
- w_res_in: bfloat16 [1024, 4096], P(None, 'mp'), may hold values from -0.1875 to 0.1875
- w_res_out: bfloat16 [4096, 1024], P('mp'), may hold values from -0.09375 to 0.09375
- w_exp_in: bfloat16 [32, 1024, 4096], P('expert', None, 'mp'), may hold values from -0.1875 to 0.1875
- w_exp_out: bfloat16 [32, 4096, 1024], P('expert', 'mp'), may hold values from -0.09375 to 0.09375
- expert_of: int32 [49152], P(('groups', 'expert')), parts along dimension 0, may hold values from 0 to 31
- slot_of: int32 [49152], P(('groups', 'expert')), parts along dimension 0, may hold values from -1 to 29, as said below
- gate_prob: float32 [49152], P(('groups', 'expert')), parts along dimension 0, may hold values from 0.2 to 1
Outputs:
- layer_out: bfloat16 [49152, 1024], P(('groups', 'expert'), 'mp'), parts along dimension 0
There are 2 independent parts, one for each index of `groups`. A program takes and returns all parts, laid end to end along the dimension named above; an argument that names none is the same for every part. Nothing has to cross between parts.
Inputs may be any that keep to these rules, and one draw needn't show every extreme that they name: slot_of[t] is the number of earlier tokens of t's aligned block of 768 tokens with the same expert_of, or -1 where that number is 30 or more. In every draw one expert has more than 30 tokens in every aligned block.
All inputs are finite; a program needn't handle non-finite values.
Results may differ from a plain program's by a relative error of at most 0.014.
Values may be sent and summed in bfloat16 or wider, within the bound.
A program may use at most 64 MiB of HBM per device.

v0:
```python
import jax
import jax.numpy as jnp
from jax import lax
from jax.sharding import PartitionSpec as P


def laid_out(parts, dim):
    parts = jnp.moveaxis(parts, 0, dim)
    dims = parts.shape
    return parts.reshape(*dims[:dim], dims[dim] * dims[dim + 1], *dims[dim + 2 :])


def from_everyone(shard, axis):
    devices = lax.axis_size(axis)
    return lax.all_to_all(
        jnp.broadcast_to(shard[None], (devices, *shard.shape)), axis, 0, 0, tiled=True
    )


def collect(shard, axis, dim):
    return laid_out(from_everyone(shard, axis), dim)


def rms_rows(tokens, gain):
    values = tokens.astype(jnp.float32)
    inverse = lax.rsqrt(jnp.mean(values * values, axis=-1, keepdims=True) + 1e-05)
    return (values * inverse * gain).astype(jnp.bfloat16)


def per_device(
    tokens, gain, w_res_in, w_res_out, w_exp_in, w_exp_out, expert_of, slot_of, gate_prob
):
    full_rows = collect(tokens, "mp", 1)
    normed = rms_rows(full_rows, gain)
    res_hidden = jax.nn.gelu(jnp.dot(normed, w_res_in, preferred_element_type=jnp.float32)).astype(
        jnp.bfloat16
    )
    res_part = jnp.dot(res_hidden, w_res_out, preferred_element_type=jnp.float32)
    row_count = expert_of.shape[0]
    experts = lax.axis_size("expert")
    capacity = max(2, 5 * row_count // (4 * experts))
    feat_width = tokens.shape[1]
    slot_id = jnp.where(slot_of >= 0, expert_of * capacity + slot_of, -1)
    slot_index = jnp.arange(experts * capacity, dtype=jnp.int32)
    send_table = (slot_index[:, None] == slot_id[None, :]).astype(jnp.bfloat16)
    take_table = (slot_id[:, None] == slot_index[None, :]).astype(jnp.bfloat16)
    local_in = w_exp_in[0]
    local_out = w_exp_out[0]
    mp_index = lax.axis_index("mp")
    own_slice = lax.dynamic_slice_in_dim(normed, mp_index * feat_width, feat_width, 1)
    outgoing = jnp.dot(send_table, own_slice, preferred_element_type=jnp.float32).astype(
        jnp.bfloat16
    )
    incoming = lax.all_to_all(
        outgoing.reshape(experts, capacity, feat_width),
        "expert",
        split_axis=0,
        concat_axis=0,
        tiled=True,
    )
    piece = collect(incoming, "mp", 2)
    flat_piece = piece.reshape(-1, piece.shape[2])
    preact = jnp.dot(flat_piece, local_in, preferred_element_type=jnp.float32)
    exp_hidden = jax.nn.gelu(preact).astype(jnp.bfloat16)
    exp_part = jnp.dot(exp_hidden, local_out, preferred_element_type=jnp.float32)
    gate_column = gate_prob[:, None]
    summed = lax.psum_scatter(exp_part.astype(jnp.bfloat16), "mp", scatter_dimension=1, tiled=True)
    returned = lax.all_to_all(
        summed.reshape(experts, capacity, feat_width),
        "expert",
        split_axis=0,
        concat_axis=0,
        tiled=True,
    )
    moe_value = jnp.dot(
        take_table,
        returned.reshape(experts * capacity, feat_width),
        preferred_element_type=jnp.float32,
    )
    res_sum = lax.psum_scatter(
        res_part.astype(jnp.bfloat16), "mp", scatter_dimension=1, tiled=True
    ).astype(jnp.float32)
    return (res_sum + gate_column * moe_value).astype(jnp.bfloat16)


def solution(mesh):
    return jax.shard_map(
        per_device,
        mesh=mesh,
        in_specs=(
            P(("groups", "expert"), "mp"),
            P(),
            P(None, "mp"),
            P("mp", None),
            P("expert", None, "mp"),
            P("expert", "mp", None),
            P(("groups", "expert")),
            P(("groups", "expert")),
            P(("groups", "expert")),
        ),
        out_specs=P(("groups", "expert"), "mp"),
        check_vma=False,
    )
```

profile of v0, /device:TPU:80, one launch (start us, length us, event | category | flops | bytes accessed | tf_op | source)
XLA Modules:
  0.0 280.3 jit_solution(4909868781733401245)
XLA Ops:
  6.5 0.0 copy-start
  6.6 1.1 copy.13
  7.7 1.3 broadcast_in_dim.8
  9.0 0.0 copy-start.4
  9.0 0.0 copy-start.5
  9.0 0.0 copy-start.3
  9.0 7.4 %all-to-all-start = ((bf16[8,768,128]{1,2,0:T(8,128)(2,1)}), bf16[8,768,128]{1,2,0:T(8,128)(2,1)S(1)}, u32[]{:S(2)}, u32[]{:S(2)}) async-start(bf16[8,768,128]{1,2,0:T(8,128)(2,1)} %broadcast_in_dim.8), calls=%async_computation | async-start | bytes 3145728 | tf_op jit(solution)/shard_map/all_to_all | solution.py:15
  16.4 0.1 reduce-scatter.9.cloned.1.call-start
  16.5 0.0 copy-done.4
  16.5 0.0 copy-done.5
  16.5 39.9 %all-to-all-done = bf16[8,768,128]{1,2,0:T(8,128)(2,1)S(1)} async-done(((bf16[8,768,128]{1,2,0:T(8,128)(2,1)}), bf16[8,768,128]{1,2,0:T(8,128)(2,1)S(1)}, u32[]{:S(2)}, u32[]{:S(2)}) %all-to-all-start) | async-done | bytes 1572896 | tf_op jit(solution)/shard_map/all_to_all | solution.py:15
  56.4 0.4 multiply_reduce_fusion
  56.8 0.0 copy-done.3
  56.8 0.4 fusion.1
  57.3 0.0 copy-start.1
  57.3 1.2 copy-done.1
  58.4 0.6 fusion.27
  59.1 0.1 reshape.26
  59.1 66.3 %all_to_all.20 = bf16[32,30,128]{2,1,0:T(8,128)(2,1)S(1)} all-to-all(bf16[32,30,128]{2,1,0:T(8,128)(2,1)S(1)} %reshape.26), channel_id=1, replica_groups=mesh['groups'=2,'expert'=32,'mp'=8] {'expert'}, dimensions={0} | all-to-all | bytes 491520 | tf_op jit(solution)/shard_map/all_to_all | solution.py:54
  125.4 0.1 copy.14
  125.5 0.3 broadcast_in_dim.10
  125.8 51.2 %all_to_all.21 = bf16[8,32,30,128]{3,1,2,0:T(8,128)(2,1)S(1)} all-to-all(bf16[8,32,30,128]{3,1,2,0:T(8,128)(2,1)S(1)} %broadcast_in_dim.10), channel_id=1, replica_groups=mesh['groups'=2,'expert'=32,'mp'=8] {'mp'}, dimensions={0} | all-to-all | bytes 3932160 | tf_op jit(solution)/shard_map/all_to_all | solution.py:15
  177.0 1.3 copy.15
  178.3 0.0 copy-done
  178.3 5.0 %convolution_convert_fusion = bf16[960,1024]{1,0:T(8,128)(2,1)} fusion(bf16[1,512,1024]{2,1,0:T(8,128)(2,1)S(1)} %copy-done, bf16[120,8,8,128]{3,2,1,0:T(8,128)(2,1)S(1)} %bitcast.37, bf16[1,1024,512]{2,1,0:T(8,128)(2,1)} %param.13), kind=kOutput, calls=%fused_computation.21 | convolution fusion | flops 2018672640 | bytes 6029312 | tf_op jit(solution)/shard_map/dot_general | solution.py:65
  183.3 3.9 %copy.18 = bf16[960,1024]{0,1:T(8,128)(2,1)} copy(bf16[960,1024]{1,0:T(8,128)(2,1)} %convolution_convert_fusion) | data formatting | bytes 3932160
  187.2 0.0 copy-start.2
  187.2 0.1 reduce-scatter.9.cloned.1.call-update
  187.2 0.1 reduce-scatter.7.cloned.1.call-start
  187.3 1.3 copy-done.2
  188.6 4.7 %convolution_convert_fusion.1 = bf16[768,1024]{1,0:T(8,128)(2,1)} fusion(bf16[512,1024]{1,0:T(8,128)(2,1)} %param.12, bf16[768,1024]{0,1:T(8,128)(2,1)S(1)} %copy-done.2, bf16[1024,512]{1,0:T(8,128)(2,1)} %param.11), kind=kOutput, calls=%fused_computation.22 | convolution fusion | flops 1614938112 | bytes 5242880 | tf_op jit(solution)/shard_map/dot_general | solution.py:38
  193.3 2.6 copy.16
  195.9 0.0 copy-start.6
  195.9 0.1 reduce-scatter.7.cloned.1.call-update
  195.9 26.2 %reduce-scatter.9.cloned.1.call-done = bf16[128,960]{1,0:T(8,128)(2,1)} async-done(((bf16[1024,960]{1,0:T(8,128)(2,1)}), bf16[128,960]{1,0:T(8,128)(2,1)}) %reduce-scatter.9.cloned.1.call-update) | async-done | bytes 245776
  222.2 1.1 copy.19
  223.3 0.8 reshape.27
  224.1 13.9 %all-to-all-start.3 = ((bf16[32,30,128]{2,1,0:T(8,128)(2,1)}), bf16[32,30,128]{2,1,0:T(8,128)(2,1)S(1)}, u32[]{:S(2)}, u32[]{:S(2)}) async-start(bf16[32,30,128]{2,1,0:T(8,128)(2,1)} %reshape.27), calls=%async_computation.3 | async-start | bytes 524288 | tf_op jit(solution)/shard_map/all_to_all | solution.py:68
  238.0 32.9 %reduce-scatter.7.cloned.1.call-done = bf16[128,768]{1,0:T(8,128)(2,1)} async-done(((bf16[1024,768]{1,0:T(8,128)(2,1)}), bf16[128,768]{1,0:T(8,128)(2,1)}) %reduce-scatter.7.cloned.1.call-update) | async-done | bytes 196624
  270.9 1.1 copy.17
  272.0 0.0 all-to-all-done.3
  272.0 0.1 reshape.28
  272.0 0.0 copy-done.6
  272.1 1.4 fusion.28
  (2 shorter events, 0.0 us)
Async XLA Ops:
  6.5 171.8 %copy-start = (bf16[1,512,1024]{2,1,0:T(8,128)(2,1)S(1)}, bf16[1,512,1024]{2,1,0:T(8,128)(2,1)}, u32[]{:S(2)}) copy-start(bf16[1,512,1024]{2,1,0:T(8,128)(2,1)} %param.14) | copy-start | bytes 3145732
  9.0 7.5 %copy-start.4 = (s32[768]{0:T(1024)S(1)}, s32[768]{0:T(1024)}, u32[]{:S(2)}) copy-start(s32[768]{0:T(1024)} %param.16) | copy-start | bytes 9220
  9.0 7.5 %copy-start.5 = (s32[768]{0:T(1024)S(1)}, s32[768]{0:T(1024)}, u32[]{:S(2)}) copy-start(s32[768]{0:T(1024)} %param.15) | copy-start | bytes 9220
  9.0 47.9 %copy-start.3 = (f32[1024]{0:T(1024)S(1)}, f32[1024]{0:T(1024)}, u32[]{:S(2)}) copy-start(f32[1024]{0:T(1024)} %param.10) | copy-start | bytes 12292
  9.0 47.5 %all-to-all-start = ((bf16[8,768,128]{1,2,0:T(8,128)(2,1)}), bf16[8,768,128]{1,2,0:T(8,128)(2,1)S(1)}, u32[]{:S(2)}, u32[]{:S(2)}) async-start(bf16[8,768,128]{1,2,0:T(8,128)(2,1)} %broadcast_in_dim.8), calls=%async_computation | async-start | bytes 3145728 | tf_op jit(solution)/shard_map/all_to_all | solution.py:15
  16.4 205.8 %reduce-scatter.9.cloned.1.call-start = ((), (), s32[]{:S(2)}) async-start(), calls=%async_computation.7 | async-start | bytes 2359296
  57.3 1.2 copy-start.1
  187.2 1.4 copy-start.2
  187.2 83.6 %reduce-scatter.7.cloned.1.call-start = ((), (), s32[]{:S(2)}) async-start(), calls=%async_computation.6 | async-start | bytes 1769472
  195.9 76.2 %copy-start.6 = (f32[768]{0:T(1024)S(1)}, f32[768]{0:T(1024)}, u32[]{:S(2)}) copy-start(f32[768]{0:T(1024)} %param.17) | copy-start | bytes 9220
  224.1 47.9 %all-to-all-start.3 = ((bf16[32,30,128]{2,1,0:T(8,128)(2,1)}), bf16[32,30,128]{2,1,0:T(8,128)(2,1)S(1)}, u32[]{:S(2)}, u32[]{:S(2)}) async-start(bf16[32,30,128]{2,1,0:T(8,128)(2,1)} %reshape.27), calls=%async_computation.3 | async-start | bytes 524288 | tf_op jit(solution)/shard_map/all_to_all | solution.py:68
Sparse Core Ops, SparseCore 0:
  187.4 34.7 reduce-scatter.8
  225.1 45.7 reduce-scatter.6
where the time goes:
time: 282 us; the launch traced here: 280 us
  blocking collectives  117 us (41%)
  waiting for transfers between devices  99.2 us (35%)
  starting transfers between devices  21.5 us (8%)
  local copies, waits for them, and re-layouts  16.2 us (6%)
  between operations  13.6 us (5%)
  matrix products  11.7 us (4%)
    all_to_all x1, blocking collectives, per_device(): lax.all_to_all(outgoing.reshape(experts, capacity, feat_width), 'expert',...  66.3 us
    unnamed x4, waiting for transfers between devices  59.2 us
    all_to_all x1, blocking collectives, from_everyone(): lax.all_to_all(jnp.broadcast_to(shard[None], (devices, *shard.shape)), ax...  51.2 us
    all_to_all x1, waiting for transfers between devices, from_everyone(): lax.all_to_all(jnp.broadcast_to(shard[None], (devices, *shard.shape)), ax...  39.9 us
    all_to_all x1, starting transfers between devices, per_device(): lax.all_to_all(summed.reshape(experts, capacity, feat_width), 'expert', s...  13.9 us
    unnamed x19, local copies, waits for them, and re-layouts  12.3 us
    all_to_all x1, starting transfers between devices, from_everyone(): lax.all_to_all(jnp.broadcast_to(shard[None], (devices, *shard.shape)), ax...  7.45 us
  transfers between devices with their start and end apart: 4, of which 3 were waited for; matrix products, arithmetic and copies ran while one was open for 4% of the time, Pallas kernels for 0%

commit v1 on v0

v1 whole, which is shorter than its diff:
```python
import functools

import jax
import jax.numpy as jnp
from jax import lax
from jax.experimental import pallas as pl
from jax.experimental.pallas import tpu as pltpu
from jax.sharding import PartitionSpec as P

MESH = pl.DeviceIdType.MESH
BF16 = jnp.bfloat16
F32 = jnp.float32


def rms_rows(pieces, gain):
    values = jnp.concatenate([piece.astype(F32) for piece in pieces], axis=1)
    inverse = lax.rsqrt(jnp.mean(values * values, axis=-1, keepdims=True) + 1e-05)
    return (values * inverse * gain).astype(BF16)


def mlp_rows(rows, w_in, w_out):
    hidden = jax.nn.gelu(jnp.dot(rows, w_in[...], preferred_element_type=F32)).astype(BF16)
    return jnp.dot(hidden, w_out[...], preferred_element_type=F32)


def remote(src, dst, send_sem, recv_sem, axis, device):
    return pltpu.make_async_remote_copy(
        src_ref=src,
        dst_ref=dst,
        send_sem=send_sem,
        recv_sem=recv_sem,
        device_id={axis: device},
        device_id_type=MESH,
    )


def layer_kernel(
    experts, ring, slots, chunks,
    meta, tok_hbm, wri_hbm, wro_hbm, wei_hbm, weo_hbm, out,
    tok_all, exp_all, outgoing, wri, wro, wei, weo, res_part, exp_part,
    rs_send, rs_recv, es_send, es_recv, ret_send, returned, table, gate_cols,
    local_sem, tok_ss, tok_rs, exp_ss, exp_rs, dis_ss, dis_rs,
    rs_ss, rs_rs, es_ss, es_rs, ret_ss, ret_rs,
):
    me = lax.axis_index("mp")
    mine = lax.axis_index("expert")
    tokens, width = out.shape
    total = experts * slots
    messages = ring - 1
    chunk_rows = total // chunks

    def on_ring(offset):
        return lax.rem(me + offset + 2 * ring, ring)

    def partner(p):
        far = lax.div(p + 1, 2)
        return experts // 2 + jnp.where(lax.rem(p, 2) == 0, far, -far)

    barrier = pltpu.get_barrier_semaphore()
    for offset in (-1, 1):
        pl.semaphore_signal(
            barrier, inc=1, device_id={"mp": on_ring(offset)}, device_id_type=MESH
        )

    def greet(step, carry):
        pl.semaphore_signal(
            barrier,
            inc=1,
            device_id={"expert": lax.rem(mine + step, experts)},
            device_id_type=MESH,
        )
        return carry

    lax.fori_loop(1, experts, greet, 0)

    tok_copy = pltpu.make_async_copy(tok_hbm, tok_all.at[me], local_sem.at[0])
    tok_copy.start()
    weight_copies = [
        pltpu.make_async_copy(src, dst, local_sem.at[1 + at])
        for at, (src, dst) in enumerate(
            ((wri_hbm, wri), (wro_hbm, wro), (wei_hbm, wei), (weo_hbm, weo))
        )
    ]
    for copy in weight_copies:
        copy.start()
    tok_copy.wait()

    slot_row = meta[0:1, 0:tokens]

    def pick(step, carry):
        rows = pl.ds(pl.multiple_of(step * chunk_rows, chunk_rows), chunk_rows)
        index = lax.broadcasted_iota(jnp.int32, (chunk_rows, tokens), 0) + step * chunk_rows
        one_hot = jnp.where(index.astype(F32) == slot_row, 1.0, 0.0).astype(BF16)
        outgoing[rows, :] = jnp.dot(
            one_hot, tok_all[me], preferred_element_type=F32
        ).astype(BF16)
        return carry

    lax.fori_loop(0, chunks, pick, 0)
    pl.semaphore_wait(barrier, experts + 1)

    def gather_copy(buf, send_sem, recv_sem, j, way, arriving):
        turn = 1 - 2 * way
        half = buf.shape[1] // 2
        shard = on_ring(-turn * (j // 2 + (1 if arriving else 0)))
        ref = buf.at[shard, pl.ds(((j + way) % 2) * half, half)]
        return remote(ref, ref, send_sem.at[way, j], recv_sem.at[way, j], "mp", on_ring(turn))

    def gather_send(ring_refs, j):
        for way in (0, 1):
            gather_copy(*ring_refs, j, way, False).start()

    def gather_step(ring_refs, j):
        for way in (0, 1):
            gather_copy(*ring_refs, j, way, True).wait_recv()
            if j + 2 < messages:
                gather_copy(*ring_refs, j + 2, way, False).start()

    tok_ring = (tok_all, tok_ss, tok_rs)
    exp_ring = (exp_all, exp_ss, exp_rs)
    gather_send(tok_ring, 0)

    def block(at):
        return pl.ds(pl.multiple_of(at * slots, slots), slots)

    def dispatch(p, carry):
        target = lax.rem(mine - partner(p) + experts, experts)
        remote(
            outgoing.at[block(target)], exp_all.at[me, block(p)],
            dis_ss.at[0], dis_rs.at[0], "expert", target,
        ).start()
        return carry

    lax.fori_loop(0, experts - 1, dispatch, 0)
    own_copy = pltpu.make_async_copy(
        outgoing.at[block(mine)], exp_all.at[me, block(experts - 1)], local_sem.at[5]
    )
    own_copy.start()
    gather_send(tok_ring, 1)

    def turned(row):
        return jnp.transpose(jnp.broadcast_to(row, (width, tokens)))

    gate_cols[...] = turned(meta[1:2, 0:tokens])
    slot_cols = turned(slot_row)
    lane = lax.broadcasted_iota(jnp.int32, (tokens, width), 1)
    for at in range(0, total, width):
        wide = min(width, total - at)
        hit = jnp.where((lane + at).astype(F32) == slot_cols, 1.0, 0.0).astype(BF16)
        table[:, at : at + wide] = hit[:, :wide]

    for j in range(messages - 2):
        gather_step(tok_ring, j)

    others = pl.ds(0, (experts - 1) * slots)

    def all_dispatched():
        return remote(
            outgoing.at[others], exp_all.at[me, others], dis_ss.at[0], dis_rs.at[0], "expert",
            lax.rem(mine + 1, experts),
        )

    own_copy.wait()
    all_dispatched().wait_recv()
    gather_send(exp_ring, 0)
    gather_send(exp_ring, 1)
    for j in range(messages - 2, messages):
        gather_step(tok_ring, j)

    gain = meta[2:3, 0 : ring * width]
    weight_copies[0].wait()
    weight_copies[1].wait()
    res_rows = tokens // 3 if tokens % 48 == 0 else tokens

    def residual(step, carry):
        rows = pl.ds(pl.multiple_of(step * res_rows, res_rows), res_rows)
        normed = rms_rows([tok_all[k, rows, :] for k in range(ring)], gain)
        part = mlp_rows(normed, wri, wro)
        for k in range(ring):
            res_part[k, rows, :] = part[:, k * width : (k + 1) * width]
        return carry

    lax.fori_loop(0, tokens // res_rows, residual, 0)

    def scatter_copy(refs, c, j, way):
        send, recv, send_sem, recv_sem = refs[1:]
        return remote(
            send.at[way, c, j], recv.at[way, c, j],
            send_sem.at[way, c, j], recv_sem.at[way, c, j], "mp", on_ring(1 - 2 * way),
        )

    def scatter_send(refs, c, j):
        part, send, recv = refs[:3]
        half = send.shape[3]
        for way in (0, 1):
            turn = 1 - 2 * way
            dest = on_ring(turn * (ring // 2 - (j + 1) // 2))
            start = pl.multiple_of(c * 2 * half + ((j + way) % 2) * half, half)
            value = part[dest, pl.ds(start, half), :]
            if j >= 2:
                scatter_copy(refs, c, j - 2, way).wait_recv()
                value = value + recv[way, c, j - 2].astype(F32)
            send[way, c, j] = value.astype(BF16)
            scatter_copy(refs, c, j, way).start()

    def scatter_sum(refs, c, h):
        part, send, recv = refs[:3]
        half = send.shape[3]
        start = pl.multiple_of(c * 2 * half + h * half, half)
        value = part[me, pl.ds(start, half), :]
        for way in (0, 1):
            j = messages - 1 if h == way else messages - 2
            scatter_copy(refs, c, j, way).wait_recv()
            value = value + recv[way, c, j].astype(F32)
        return value

    res_sums = (res_part, rs_send, rs_recv, rs_ss, rs_rs)
    exp_sums = (exp_part, es_send, es_recv, es_ss, es_rs)

    for j in range(messages - 2):
        gather_step(exp_ring, j)
    scatter_send(res_sums, 0, 0)
    scatter_send(res_sums, 0, 1)
    for j in range(messages - 2, messages):
        gather_step(exp_ring, j)

    weight_copies[2].wait()
    weight_copies[3].wait()

    def expert(c, carry):
        rows = pl.ds(pl.multiple_of(c * chunk_rows, chunk_rows), chunk_rows)
        normed = rms_rows([exp_all[k, rows, :] for k in range(ring)], gain)
        part = mlp_rows(normed, wei, weo)
        for k in range(ring):
            exp_part[k, rows, :] = part[:, k * width : (k + 1) * width]
        scatter_send(exp_sums, c, 0)
        scatter_send(exp_sums, c, 1)
        return carry

    lax.fori_loop(0, chunks, expert, 0)

    for j in range(2, messages):

        def wave(c, carry, j=j):
            scatter_send(exp_sums, c, j)
            return carry

        lax.fori_loop(0, chunks, wave, 0)

    early = min(4, messages)
    for j in range(2, early):
        scatter_send(res_sums, 0, j)

    def give_back(p, carry):
        source = lax.rem(mine + partner(p), experts)
        remote(
            ret_send.at[block(p)], returned.at[block(mine)],
            ret_ss.at[0], ret_rs.at[0], "expert", source,
        ).start()
        return carry

    per_chunk = experts // chunks
    half_rows = chunk_rows // 2
    for c in range(chunks):
        for h in (0, 1):
            ret_send[pl.ds(c * chunk_rows + h * half_rows, half_rows), :] = scatter_sum(
                exp_sums, c, h
            ).astype(BF16)
        last = experts - 1 if c == chunks - 1 else (c + 1) * per_chunk
        lax.fori_loop(c * per_chunk, last, give_back, 0)
    own_back = pltpu.make_async_copy(
        ret_send.at[block(experts - 1)], returned.at[block(mine)], local_sem.at[5]
    )
    own_back.start()

    for j in range(early, messages):
        scatter_send(res_sums, 0, j)
    half = tokens // 2
    sums = [scatter_sum(res_sums, 0, h) for h in (0, 1)]

    own_back.wait()

    def all_returned():
        return remote(
            ret_send.at[others], returned.at[others], ret_ss.at[0], ret_rs.at[0], "expert",
            lax.rem(mine + 1, experts),
        )

    all_returned().wait_recv()
    for h in (0, 1):
        rows = pl.ds(h * half, half)
        moe = jnp.dot(table[rows, :], returned[...], preferred_element_type=F32)
        out[rows, :] = (sums[h] + gate_cols[rows, :] * moe).astype(BF16)

    all_dispatched().wait_send()
    all_returned().wait_send()
    for j in range(messages):
        for way in (0, 1):
            gather_copy(*tok_ring, j, way, False).wait_send()
            gather_copy(*exp_ring, j, way, False).wait_send()
            scatter_copy(res_sums, 0, j, way).wait_send()

    def drain(c, carry):
        for j in range(messages):
            for way in (0, 1):
                scatter_copy(exp_sums, c, j, way).wait_send()
        return carry

    lax.fori_loop(0, chunks, drain, 0)


def per_device(
    experts, ring, tokens, gain, w_res_in, w_res_out, w_exp_in, w_exp_out,
    expert_of, slot_of, gate_prob,
):
    count, width = tokens.shape
    model, hidden = w_res_in.shape
    capacity = max(2, 5 * count // (4 * experts))
    slots = -(-capacity // 16) * 16
    chunks = 4
    total = experts * slots
    messages = ring - 1

    slot_id = jnp.where(slot_of >= 0, expert_of * slots + slot_of, -1).astype(F32)
    span = max(count, model)
    meta = jnp.stack(
        [
            jnp.pad(slot_id, (0, span - count)),
            jnp.pad(gate_prob, (0, span - count)),
            jnp.pad(gain, (0, span - model)),
        ]
    )
    any_space = pl.BlockSpec(memory_space=pl.ANY)
    in_vmem = pl.BlockSpec(memory_space=pltpu.VMEM)
    sems = pltpu.SemaphoreType.DMA
    res_half, exp_half = count // 2, total // chunks // 2
    return pl.pallas_call(
        functools.partial(layer_kernel, experts, ring, slots, chunks),
        out_shape=jax.ShapeDtypeStruct((count, width), BF16),
        in_specs=[in_vmem] + [any_space] * 5,
        out_specs=in_vmem,
        scratch_shapes=[
            pltpu.VMEM((ring, count, width), BF16),
            pltpu.VMEM((ring, total, width), BF16),
            pltpu.VMEM((total, width), BF16),
            pltpu.VMEM((model, hidden), BF16),
            pltpu.VMEM((hidden, model), BF16),
            pltpu.VMEM((model, hidden), BF16),
            pltpu.VMEM((hidden, model), BF16),
            pltpu.VMEM((ring, count, width), F32),
            pltpu.VMEM((ring, total, width), F32),
            pltpu.VMEM((2, 1, messages, res_half, width), BF16),
            pltpu.VMEM((2, 1, messages, res_half, width), BF16),
            pltpu.VMEM((2, chunks, messages, exp_half, width), BF16),
            pltpu.VMEM((2, chunks, messages, exp_half, width), BF16),
            pltpu.VMEM((total, width), BF16),
            pltpu.VMEM((total, width), BF16),
            pltpu.VMEM((count, total), BF16),
            pltpu.VMEM((count, width), F32),
            sems((6,)),
            sems((2, messages)),
            sems((2, messages)),
            sems((2, messages)),
            sems((2, messages)),
            sems((1,)),
            sems((1,)),
            sems((2, 1, messages)),
            sems((2, 1, messages)),
            sems((2, chunks, messages)),
            sems((2, chunks, messages)),
            sems((1,)),
            sems((1,)),
        ],
        compiler_params=pltpu.CompilerParams(
            collective_id=0, has_side_effects=True, vmem_limit_bytes=56 * 1024 * 1024
        ),
        name="moe_layer",
    )(meta, tokens, w_res_in, w_res_out, w_exp_in[0], w_exp_out[0])


def solution(mesh):
    return jax.shard_map(
        functools.partial(per_device, mesh.shape["expert"], mesh.shape["mp"]),
        mesh=mesh,
        in_specs=(
            P(("groups", "expert"), "mp"),
            P(),
            P(None, "mp"),
            P("mp", None),
            P("expert", None, "mp"),
            P("expert", "mp", None),
            P(("groups", "expert")),
            P(("groups", "expert")),
            P(("groups", "expert")),
        ),
        out_specs=P(("groups", "expert"), "mp"),
        check_vma=False,
    )
```

time: 282 us -> 128 us (0.45)
  Pallas kernels: 0 us -> 123 us
  blocking collectives: 117 us -> 0 us
  waiting for transfers between devices: 99.2 us -> 0 us
  starting transfers between devices: 21.5 us -> 0 us
  between operations: 13.6 us -> 0.01 us
  local copies, waits for them, and re-layouts: 16.2 us -> 3.67 us
  matrix products: 11.7 us -> 0 us
    pallas_call x0 -> x1, Pallas kernels: none -> 123 us  [per_device(): pl.pallas_call(functools.partial(layer_kernel, experts, ring, slots, chun...]
    all_to_all x2 -> x0, blocking collectives: 117 us -> none  [the longest x1 66.3 us: per_device(): lax.all_to_all(outgoing.reshape(experts, capacity, feat_width), 'expert',...]
    unnamed x4 -> x0, waiting for transfers between devices: 59.2 us -> none
    all_to_all x2 -> x0, waiting for transfers between devices: 39.9 us -> none  [the longest x1 39.9 us: from_everyone(): lax.all_to_all(jnp.broadcast_to(shard[None], (devices, *shard.shape)), ax...]
    all_to_all x2 -> x0, starting transfers between devices: 21.3 us -> none  [the longest x1 13.9 us: per_device(): lax.all_to_all(summed.reshape(experts, capacity, feat_width), 'expert', s...]
    dot_general x4 -> x0, matrix products: 11.7 us -> none  [the longest x1 4.96 us: per_device(): jnp.dot(exp_hidden, local_out, preferred_element_type=jnp.float32)]
    unnamed x19 -> x7, local copies, waits for them, and re-layouts: 12.3 us -> 3.67 us
  transfers between devices with their start and end apart: 4 -> 0, of which waited for: 3 -> 0; matrix products, arithmetic and copies ran while one was open for 4% -> 0% of each run, Pallas kernels for 0% -> 0%
where the time goes in v1:
time: 128 us
  Pallas kernels  123 us (96%)
  local copies, waits for them, and re-layouts  3.67 us (3%)
  other arithmetic  1.31 us (1%)
    pallas_call x1, Pallas kernels, per_device(): pl.pallas_call(functools.partial(layer_kernel, experts, ring, slots, chun...  123 us
    unnamed x7, local copies, waits for them, and re-layouts  3.67 us

profile of v1, /device:TPU:80, one launch (start us, length us, event | category | flops | bytes accessed | tf_op | source)
XLA Modules:
  0.0 127.8 jit_solution(16039827260544274867)
XLA Ops:
  0.0 0.0 copy-start
  0.0 0.7 copy-done
  0.7 0.7 select_convert_fusion
  1.4 0.0 copy-start.2
  1.4 0.7 copy-done.2
  2.1 0.0 copy-start.1
  2.1 0.7 copy-done.1
  2.8 0.6 pad_maximum_fusion.meta
  3.4 122.8 %moe_layer.1 = bf16[768,128]{1,0:T(8,128)(2,1)} custom-call(f32[3,1024]{1,0:T(4,128)} %pad_maximum_fusion.meta, bf16[768,128]{1,0:T(8,128)(2,1)} %tok_hbm.1, bf16[1024,512]{1,0:T(8,128)(2,1)} %wri_hbm.1, bf16[512,1024]{1,0:T(8,128)(2,1)} %wro_hbm.1, bf16[1024,512]{1,0:T(8,128)(2,1)} %bitcast.5, bf16[512,1024]{1,0:T(8,128)(2,1)} %bitcast.6), custom_call_target="tpu_custom_call" | custom-call | tf_op jit(solution)/shard_map/moe_layer/pallas_call | solution.py:337
  126.2 1.6 %copy.11 = bf16[768,128]{1,0:T(8,128)(2,1)} copy(bf16[768,128]{1,0:T(8,128)(2,1)} %moe_layer.1) | data formatting | bytes 393216
  (2 shorter events, 0.0 us)
Async XLA Ops:
  0.0 0.7 copy-start
  1.4 0.7 copy-start.2
  2.1 0.7 copy-start.1

commit v2 on v1

v2 whole, which is shorter than its diff:
```python
import functools

import jax
import jax.numpy as jnp
from jax import lax
from jax.experimental import pallas as pl
from jax.experimental.pallas import tpu as pltpu
from jax.sharding import PartitionSpec as P

MESH = pl.DeviceIdType.MESH
BF16 = jnp.bfloat16
F32 = jnp.float32


def rms_rows(pieces, gain):
    values = jnp.concatenate([piece.astype(F32) for piece in pieces], axis=1)
    inverse = lax.rsqrt(jnp.mean(values * values, axis=-1, keepdims=True) + 1e-05)
    return (values * inverse * gain).astype(BF16)


def mlp_rows(rows, w_in, w_out):
    hidden = jax.nn.gelu(jnp.dot(rows, w_in[...], preferred_element_type=F32)).astype(BF16)
    return jnp.dot(hidden, w_out[...], preferred_element_type=F32)


def remote(src, dst, send_sem, recv_sem, axis, device):
    return pltpu.make_async_remote_copy(
        src_ref=src,
        dst_ref=dst,
        send_sem=send_sem,
        recv_sem=recv_sem,
        device_id={axis: device},
        device_id_type=MESH,
    )


def layer_kernel(
    experts, ring, slots, chunks,
    ids_hbm, slots_hbm, gate_hbm, gain_hbm, tok_hbm, wri_hbm, wro_hbm, wei_hbm, weo_hbm, out,
    ids, slot, gate, gain_row, tok_all, exp_all, outgoing, near_out, wri, wro, wei, weo,
    res_part, exp_part, rs_send, rs_recv, es_send, es_recv, ret_send, returned,
    near_ret, near_in, table, gate_cols,
    local_sem, tok_ss, tok_rs, exp_ss, exp_rs, dis_ss, dis_rs,
    rs_ss, rs_rs, es_ss, es_rs, ret_ss, ret_rs,
):
    me = lax.axis_index("mp")
    mine = lax.axis_index("expert")
    tokens, width = out.shape
    total = experts * slots
    messages = ring - 1
    chunk_rows = total // chunks
    per_chunk = experts // chunks
    far_blocks = experts - per_chunk
    far_rows = total - chunk_rows

    def on_ring(offset):
        return lax.rem(me + offset + 2 * ring, ring)

    def partner(p):
        far = lax.div(p + 1, 2)
        return experts // 2 + jnp.where(lax.rem(p, 2) == 0, far, -far)

    def expert_at(p):
        return lax.rem(mine - partner(p) + experts, experts)

    def source_at(p):
        return lax.rem(mine + partner(p), experts)

    def block(at):
        return pl.ds(pl.multiple_of(at * slots, slots), slots)

    def blocks(first, count):
        return pl.ds(first * slots, count * slots)

    barrier = pltpu.get_barrier_semaphore()
    for offset in (-1, 1):
        pl.semaphore_signal(
            barrier, inc=1, device_id={"mp": on_ring(offset)}, device_id_type=MESH
        )

    def greet(step, carry):
        pl.semaphore_signal(
            barrier,
            inc=1,
            device_id={"expert": lax.rem(mine + step, experts)},
            device_id_type=MESH,
        )
        return carry

    lax.fori_loop(1, experts, greet, 0)

    tok_copy = pltpu.make_async_copy(tok_hbm, tok_all.at[me], local_sem.at[0])
    tok_copy.start()
    small_copies = [
        pltpu.make_async_copy(src, dst, local_sem.at[7 + at])
        for at, (src, dst) in enumerate(
            ((ids_hbm, ids), (slots_hbm, slot), (gate_hbm, gate), (gain_hbm, gain_row))
        )
    ]
    for copy in small_copies:
        copy.start()
    weight_copies = [
        pltpu.make_async_copy(src, dst, local_sem.at[1 + at])
        for at, (src, dst) in enumerate(
            ((wri_hbm, wri), (wro_hbm, wro), (wei_hbm, wei), (weo_hbm, weo))
        )
    ]
    for copy in weight_copies:
        copy.start()
    for copy in small_copies:
        copy.wait()
    tok_copy.wait()
    pl.semaphore_wait(barrier, experts + 1)

    def gather_copy(refs, j, way, arriving):
        buf, rows, send_sem, recv_sem = refs
        turn = 1 - 2 * way
        half = rows // 2
        shard = on_ring(-turn * (j // 2 + (1 if arriving else 0)))
        ref = buf.at[shard, pl.ds(((j + way) % 2) * half, half)]
        return remote(ref, ref, send_sem.at[way, j], recv_sem.at[way, j], "mp", on_ring(turn))

    def gather_send(refs, j):
        for way in (0, 1):
            gather_copy(refs, j, way, False).start()

    def gather_step(refs, j):
        for way in (0, 1):
            gather_copy(refs, j, way, True).wait_recv()
            if j + 2 < messages:
                gather_copy(refs, j + 2, way, False).start()

    tok_ring = (tok_all, tokens, tok_ss, tok_rs)
    exp_ring = (exp_all, far_rows, exp_ss, exp_rs)
    gather_send(tok_ring, 0)
    gather_send(tok_ring, 1)

    def as_row(values):
        return jnp.concatenate([values[at : at + 1] for at in range(values.shape[0])], axis=1)

    slot_row = as_row(jnp.where(slot[...] >= 0, ids[...] * slots + slot[...], -1))

    def send_hits(c):
        step = lax.broadcasted_iota(jnp.int32, (slots, tokens), 0)
        hits = [
            jnp.where(step + expert_at(c * per_chunk + at) * slots == slot_row, 1.0, 0.0)
            for at in range(per_chunk)
        ]
        return jnp.concatenate(hits, axis=0).astype(BF16)

    def dispatch(p, carry):
        remote(
            outgoing.at[block(p)], exp_all.at[me, block(p)],
            dis_ss.at[0], dis_rs.at[0], "expert", expert_at(p),
        ).start()
        return carry

    def pick(c, carry):
        rows = pl.ds(pl.multiple_of(c * chunk_rows, chunk_rows), chunk_rows)
        outgoing[rows, :] = jnp.dot(
            send_hits(c), tok_all[me], preferred_element_type=F32
        ).astype(BF16)
        return lax.fori_loop(c * per_chunk, (c + 1) * per_chunk, dispatch, carry)

    lax.fori_loop(0, chunks - 1, pick, 0)

    def turned(row):
        return jnp.transpose(jnp.broadcast_to(row, (width, tokens)))

    gate_cols[...] = turned(as_row(gate[...]))
    slot_cols = turned(slot_row.astype(F32))
    lane = lax.broadcasted_iota(jnp.int32, (1, total), 1)
    wanted = jnp.zeros((1, total), jnp.int32)
    for p in range(experts):
        inside = jnp.logical_and(lane >= p * slots, lane < (p + 1) * slots)
        wanted = jnp.where(inside, lane + (expert_at(p) - p) * slots, wanted)
    wanted = wanted.astype(F32)
    for at in range(0, total, width):
        wide = min(width, total - at)
        hit = jnp.where(slot_cols[:, :wide] == wanted[:, at : at + wide], 1.0, 0.0)
        table[:, at : at + wide] = hit.astype(BF16)

    for j in range(messages - 2):
        gather_step(tok_ring, j)

    far = blocks(0, far_blocks)

    def all_dispatched():
        return remote(
            outgoing.at[far], exp_all.at[me, far], dis_ss.at[0], dis_rs.at[0], "expert",
            lax.rem(mine + 1, experts),
        )

    all_dispatched().wait_recv()
    gather_send(exp_ring, 0)
    gather_send(exp_ring, 1)
    for j in range(messages - 2, messages):
        gather_step(tok_ring, j)

    near_hits = send_hits(chunks - 1)
    for k in range(ring):
        near_out[k] = jnp.dot(near_hits, tok_all[k], preferred_element_type=F32).astype(BF16)

    def dispatch_near(p, carry):
        remote(
            near_out.at[:, block(p - far_blocks), :], exp_all.at[:, block(p), :],
            dis_ss.at[1], dis_rs.at[1], "expert", expert_at(p),
        ).start()
        return carry

    lax.fori_loop(far_blocks, experts - 1, dispatch_near, 0)
    own_copy = pltpu.make_async_copy(
        near_out.at[:, blocks(per_chunk - 1, 1), :],
        exp_all.at[:, blocks(experts - 1, 1), :],
        local_sem.at[5],
    )
    own_copy.start()

    def all_near():
        return remote(
            near_out.at[:, blocks(0, per_chunk - 1), :],
            exp_all.at[:, blocks(far_blocks, per_chunk - 1), :],
            dis_ss.at[1], dis_rs.at[1], "expert", lax.rem(mine + 1, experts),
        )

    gain = gain_row[...]
    weight_copies[0].wait()
    weight_copies[1].wait()
    tiles = 3 if tokens % 48 == 0 else 1
    res_rows = tokens // tiles
    for tile in range(tiles):
        rows = pl.ds(tile * res_rows, res_rows)
        normed = rms_rows([tok_all[k, rows, :] for k in range(ring)], gain)
        part = mlp_rows(normed, wri, wro)
        for k in range(ring):
            res_part[k, rows, :] = part[:, k * width : (k + 1) * width]
        if tile < messages - 3:
            gather_step(exp_ring, tile)
    done = min(tiles, messages - 3)

    def expert_rows(c):
        rows = pl.ds(pl.multiple_of(c * chunk_rows, chunk_rows), chunk_rows)
        normed = rms_rows([exp_all[k, rows, :] for k in range(ring)], gain)
        return rows, mlp_rows(normed, wei, weo)

    weight_copies[2].wait()
    weight_copies[3].wait()
    own_copy.wait()
    all_near().wait_recv()
    near_ret[...] = expert_rows(chunks - 1)[1].astype(BF16)

    def give_near(p, carry):
        remote(
            near_ret.at[block(p - far_blocks)], near_in.at[block(p - far_blocks)],
            ret_ss.at[1], ret_rs.at[1], "expert", source_at(p),
        ).start()
        return carry

    lax.fori_loop(far_blocks, experts - 1, give_near, 0)
    last_block = blocks(per_chunk - 1, 1)
    own_back = pltpu.make_async_copy(
        near_ret.at[last_block], near_in.at[last_block], local_sem.at[6]
    )
    own_back.start()

    def all_near_back():
        others = blocks(0, per_chunk - 1)
        return remote(
            near_ret.at[others], near_in.at[others], ret_ss.at[1], ret_rs.at[1], "expert",
            lax.rem(mine + 1, experts),
        )

    for j in range(done, messages):
        gather_step(exp_ring, j)

    def scatter_copy(refs, c, j, way):
        send, recv, send_sem, recv_sem = refs[1:]
        return remote(
            send.at[way, c, j], recv.at[way, c, j],
            send_sem.at[way, c, j], recv_sem.at[way, c, j], "mp", on_ring(1 - 2 * way),
        )

    def scatter_send(refs, c, j):
        part, send, recv = refs[:3]
        half = send.shape[3]
        for way in (0, 1):
            turn = 1 - 2 * way
            dest = on_ring(turn * (ring // 2 - (j + 1) // 2))
            start = pl.multiple_of(c * 2 * half + ((j + way) % 2) * half, half)
            value = part[dest, pl.ds(start, half), :]
            if j >= 2:
                scatter_copy(refs, c, j - 2, way).wait_recv()
                value = value + recv[way, c, j - 2].astype(F32)
            send[way, c, j] = value.astype(BF16)
            scatter_copy(refs, c, j, way).start()

    def scatter_sum(refs, c, h):
        part, send, recv = refs[:3]
        half = send.shape[3]
        start = pl.multiple_of(c * 2 * half + h * half, half)
        value = part[me, pl.ds(start, half), :]
        for way in (0, 1):
            j = messages - 1 if h == way else messages - 2
            scatter_copy(refs, c, j, way).wait_recv()
            value = value + recv[way, c, j].astype(F32)
        return value

    res_sums = (res_part, rs_send, rs_recv, rs_ss, rs_rs)
    exp_sums = (exp_part, es_send, es_recv, es_ss, es_rs)

    def expert(c, carry):
        rows, part = expert_rows(c)
        for k in range(ring):
            exp_part[k, rows, :] = part[:, k * width : (k + 1) * width]
        scatter_send(exp_sums, c, 0)
        scatter_send(exp_sums, c, 1)
        return carry

    lax.fori_loop(0, chunks - 1, expert, 0)

    def wave(j):
        def one(c, carry):
            scatter_send(exp_sums, c, j)
            return carry

        lax.fori_loop(0, chunks - 1, one, 0)

    wave(2)

    own_back.wait()
    all_near_back().wait_recv()
    near_rows = pl.ds(far_rows, chunk_rows)
    for tile in range(tiles):
        rows = pl.ds(tile * res_rows, res_rows)
        back = jnp.dot(table[rows, near_rows], near_in[...], preferred_element_type=F32)
        gates = gate_cols[rows, :]
        for k in range(ring):
            res_part[k, rows, :] += gates * back[:, k * width : (k + 1) * width]
    scatter_send(res_sums, 0, 0)
    scatter_send(res_sums, 0, 1)

    for j in range(3, messages):
        wave(j)
    early = min(4, messages)
    for j in range(2, early):
        scatter_send(res_sums, 0, j)

    def give_back(p, carry):
        remote(
            ret_send.at[block(p)], returned.at[block(p)],
            ret_ss.at[0], ret_rs.at[0], "expert", source_at(p),
        ).start()
        return carry

    half_rows = chunk_rows // 2
    for c in range(chunks - 1):
        for h in (0, 1):
            ret_send[pl.ds(c * chunk_rows + h * half_rows, half_rows), :] = scatter_sum(
                exp_sums, c, h
            ).astype(BF16)
        lax.fori_loop(c * per_chunk, (c + 1) * per_chunk, give_back, 0)

    for j in range(early, messages):
        scatter_send(res_sums, 0, j)

    def all_returned():
        return remote(
            ret_send.at[far], returned.at[far], ret_ss.at[0], ret_rs.at[0], "expert",
            lax.rem(mine + 1, experts),
        )

    all_returned().wait_recv()
    half = tokens // 2
    for h in (1, 0):
        rows = pl.ds(h * half, half)
        moe = jnp.dot(table[rows, pl.ds(0, far_rows)], returned[...], preferred_element_type=F32)
        gated = gate_cols[rows, :] * moe
        out[rows, :] = (scatter_sum(res_sums, 0, h) + gated).astype(BF16)

    all_dispatched().wait_send()
    all_near().wait_send()
    all_near_back().wait_send()
    all_returned().wait_send()
    for j in range(messages):
        for way in (0, 1):
            gather_copy(tok_ring, j, way, False).wait_send()
            gather_copy(exp_ring, j, way, False).wait_send()
            scatter_copy(res_sums, 0, j, way).wait_send()

    def drain(c, carry):
        for j in range(messages):
            for way in (0, 1):
                scatter_copy(exp_sums, c, j, way).wait_send()
        return carry

    lax.fori_loop(0, chunks - 1, drain, 0)


def per_device(
    experts, ring, tokens, gain, w_res_in, w_res_out, w_exp_in, w_exp_out,
    expert_of, slot_of, gate_prob,
):
    count, width = tokens.shape
    model, hidden = w_res_in.shape
    capacity = max(2, 5 * count // (4 * experts))
    slots = -(-capacity // 16) * 16
    chunks = 4 if experts % 8 == 0 else 2
    total = experts * slots
    messages = ring - 1
    near_rows = total // chunks
    far_rows = total - near_rows

    any_space = pl.BlockSpec(memory_space=pl.ANY)
    in_vmem = pl.BlockSpec(memory_space=pltpu.VMEM)
    sems = pltpu.SemaphoreType.DMA
    res_half, exp_half = count // 2, total // chunks // 2
    return pl.pallas_call(
        functools.partial(layer_kernel, experts, ring, slots, chunks),
        out_shape=jax.ShapeDtypeStruct((count, width), BF16),
        in_specs=[any_space] * 9,
        out_specs=in_vmem,
        scratch_shapes=[
            pltpu.VMEM((count // width, width), jnp.int32),
            pltpu.VMEM((count // width, width), jnp.int32),
            pltpu.VMEM((count // width, width), F32),
            pltpu.VMEM((1, model), F32),
            pltpu.VMEM((ring, count, width), BF16),
            pltpu.VMEM((ring, total, width), BF16),
            pltpu.VMEM((far_rows, width), BF16),
            pltpu.VMEM((ring, near_rows, width), BF16),
            pltpu.VMEM((model, hidden), BF16),
            pltpu.VMEM((hidden, model), BF16),
            pltpu.VMEM((model, hidden), BF16),
            pltpu.VMEM((hidden, model), BF16),
            pltpu.VMEM((ring, count, width), F32),
            pltpu.VMEM((ring, far_rows, width), F32),
            pltpu.VMEM((2, 1, messages, res_half, width), BF16),
            pltpu.VMEM((2, 1, messages, res_half, width), BF16),
            pltpu.VMEM((2, chunks - 1, messages, exp_half, width), BF16),
            pltpu.VMEM((2, chunks - 1, messages, exp_half, width), BF16),
            pltpu.VMEM((far_rows, width), BF16),
            pltpu.VMEM((far_rows, width), BF16),
            pltpu.VMEM((near_rows, model), BF16),
            pltpu.VMEM((near_rows, model), BF16),
            pltpu.VMEM((count, total), BF16),
            pltpu.VMEM((count, width), F32),
            sems((11,)),
            sems((2, messages)),
            sems((2, messages)),
            sems((2, messages)),
            sems((2, messages)),
            sems((2,)),
            sems((2,)),
            sems((2, 1, messages)),
            sems((2, 1, messages)),
            sems((2, chunks - 1, messages)),
            sems((2, chunks - 1, messages)),
            sems((2,)),
            sems((2,)),
        ],
        compiler_params=pltpu.CompilerParams(
            collective_id=0, has_side_effects=True, vmem_limit_bytes=56 * 1024 * 1024
        ),
        name="moe_layer",
    )(
        expert_of.reshape(-1, width), slot_of.reshape(-1, width), gate_prob.reshape(-1, width),
        gain.reshape(1, model), tokens, w_res_in, w_res_out, w_exp_in[0], w_exp_out[0],
    )


def solution(mesh):
    return jax.shard_map(
        functools.partial(per_device, mesh.shape["expert"], mesh.shape["mp"]),
        mesh=mesh,
        in_specs=(
            P(("groups", "expert"), "mp"),
            P(),
            P(None, "mp"),
            P("mp", None),
            P("expert", None, "mp"),
            P("expert", "mp", None),
            P(("groups", "expert")),
            P(("groups", "expert")),
            P(("groups", "expert")),
        ),
        out_specs=P(("groups", "expert"), "mp"),
        check_vma=False,
    )
```

time: 128 us -> 122 us (0.953)
  Pallas kernels: 123 us -> 119 us
  local copies, waits for them, and re-layouts: 3.67 us -> 1.62 us
  other arithmetic: 1.31 us -> 0 us
    pallas_call x1, Pallas kernels: 123 us -> 119 us  [per_device(): pl.pallas_call(functools.partial(layer_kernel, experts, ring, slots, chun...]
    unnamed x7 -> x1, local copies, waits for them, and re-layouts: 3.67 us -> 1.62 us
where the time goes in v2:
time: 122 us; the launch traced here: 121 us
  Pallas kernels  119 us (98%)
  local copies, waits for them, and re-layouts  1.62 us (1%)
    pallas_call x1, Pallas kernels, per_device(): pl.pallas_call(functools.partial(layer_kernel, experts, ring, slots, chun...  119 us

profile of v2, /device:TPU:80, one launch (start us, length us, event | category | flops | bytes accessed | tf_op | source)
XLA Modules:
  0.0 120.8 jit_solution(4180892579723352134)
XLA Ops:
  0.0 119.2 %moe_layer.1 = bf16[768,128]{1,0:T(8,128)(2,1)} custom-call(s32[6,128]{1,0:T(8,128)} %bitcast.8, s32[6,128]{1,0:T(8,128)} %bitcast.9, f32[6,128]{1,0:T(8,128)} %bitcast.10, f32[1,1024]{1,0:T(1,128)} %bitcast.11, bf16[768,128]{1,0:T(8,128)(2,1)} %tok_hbm.1, bf16[1024,512]{1,0:T(8,128)(2,1)} %wri_hbm.1, bf16[512,1024]{1,0:T(8,128)(2,1)} %wro_hbm.1, ...), custom_call_target="tpu_custom_call" | custom-call | tf_op jit(solution)/shard_map/moe_layer/pallas_call | solution.py:417
  119.2 1.6 %copy.11 = bf16[768,128]{1,0:T(8,128)(2,1)} copy(bf16[768,128]{1,0:T(8,128)(2,1)} %moe_layer.1) | data formatting | bytes 393216

commit v3 on v2

--- a/solution.py
+++ b/solution.py
@@ -50,8 +50,12 @@
     messages = ring - 1
     chunk_rows = total // chunks
     per_chunk = experts // chunks
-    far_blocks = experts - per_chunk
-    far_rows = total - chunk_rows
+    near_blocks = per_chunk
+    mid_blocks = per_chunk // 2
+    far_blocks = experts - near_blocks
+    ring_blocks = far_blocks - mid_blocks
+    far_rows = far_blocks * slots
+    ring_rows = ring_blocks * slots
 
     def on_ring(offset):
         return lax.rem(me + offset + 2 * ring, ring)
@@ -71,6 +75,9 @@
 
     def blocks(first, count):
         return pl.ds(first * slots, count * slots)
+
+    tok_copy = pltpu.make_async_copy(tok_hbm, tok_all.at[me], local_sem.at[0])
+    tok_copy.start()
 
     barrier = pltpu.get_barrier_semaphore()
     for offset in (-1, 1):
@@ -89,8 +96,6 @@
 
     lax.fori_loop(1, experts, greet, 0)
 
-    tok_copy = pltpu.make_async_copy(tok_hbm, tok_all.at[me], local_sem.at[0])
-    tok_copy.start()
     small_copies = [
         pltpu.make_async_copy(src, dst, local_sem.at[7 + at])
         for at, (src, dst) in enumerate(
@@ -131,7 +136,7 @@
                 gather_copy(refs, j + 2, way, False).start()
 
     tok_ring = (tok_all, tokens, tok_ss, tok_rs)
-    exp_ring = (exp_all, far_rows, exp_ss, exp_rs)
+    exp_ring = (exp_all, ring_rows, exp_ss, exp_rs)
     gather_send(tok_ring, 0)
     gather_send(tok_ring, 1)
 
@@ -140,11 +145,11 @@
 
     slot_row = as_row(jnp.where(slot[...] >= 0, ids[...] * slots + slot[...], -1))
 
-    def send_hits(c):
+    def send_hits(first, count):
         step = lax.broadcasted_iota(jnp.int32, (slots, tokens), 0)
         hits = [
-            jnp.where(step + expert_at(c * per_chunk + at) * slots == slot_row, 1.0, 0.0)
-            for at in range(per_chunk)
+            jnp.where(step + expert_at(first + at) * slots == slot_row, 1.0, 0.0)
+            for at in range(count)
         ]
         return jnp.concatenate(hits, axis=0).astype(BF16)
 
@@ -155,14 +160,16 @@
         ).start()
         return carry
 
+    group = mid_blocks
+
     def pick(c, carry):
-        rows = pl.ds(pl.multiple_of(c * chunk_rows, chunk_rows), chunk_rows)
+        rows = pl.ds(pl.multiple_of(c * group * slots, slots), group * slots)
         outgoing[rows, :] = jnp.dot(
-            send_hits(c), tok_all[me], preferred_element_type=F32
+            send_hits(c * group, group), tok_all[me], preferred_element_type=F32
         ).astype(BF16)
-        return lax.fori_loop(c * per_chunk, (c + 1) * per_chunk, dispatch, carry)
-
-    lax.fori_loop(0, chunks - 1, pick, 0)
+        return lax.fori_loop(c * group, (c + 1) * group, dispatch, carry)
+
+    lax.fori_loop(0, ring_blocks // group, pick, 0)
 
     def turned(row):
         return jnp.transpose(jnp.broadcast_to(row, (width, tokens)))
@@ -183,12 +190,13 @@
     for j in range(messages - 2):
         gather_step(tok_ring, j)
 
+    anyone = lax.rem(mine + 1, experts)
     far = blocks(0, far_blocks)
+    ringed = blocks(0, ring_blocks)
 
     def all_dispatched():
         return remote(
-            outgoing.at[far], exp_all.at[me, far], dis_ss.at[0], dis_rs.at[0], "expert",
-            lax.rem(mine + 1, experts),
+            outgoing.at[ringed], exp_all.at[me, ringed], dis_ss.at[0], dis_rs.at[0], "expert", anyone,
         )
 
     all_dispatched().wait_recv()
@@ -197,31 +205,41 @@
     for j in range(messages - 2, messages):
         gather_step(tok_ring, j)
 
-    near_hits = send_hits(chunks - 1)
-    for k in range(ring):
-        near_out[k] = jnp.dot(near_hits, tok_all[k], preferred_element_type=F32).astype(BF16)
-
-    def dispatch_near(p, carry):
-        remote(
-            near_out.at[:, block(p - far_blocks), :], exp_all.at[:, block(p), :],
-            dis_ss.at[1], dis_rs.at[1], "expert", expert_at(p),
-        ).start()
-        return carry
-
-    lax.fori_loop(far_blocks, experts - 1, dispatch_near, 0)
+    def whole_copy(first, count, sem, target):
+        return remote(
+            near_out.at[:, pl.ds(pl.multiple_of((first - ring_blocks) * slots, slots), count * slots), :],
+            exp_all.at[:, pl.ds(pl.multiple_of(first * slots, slots), count * slots), :],
+            dis_ss.at[sem], dis_rs.at[sem], "expert", target,
+        )
+
+    def dispatch_whole(first, count, last, sem):
+        hits = send_hits(first, count)
+        rows = pl.ds((first - ring_blocks) * slots, count * slots)
+        for k in range(ring):
+            near_out[k, rows, :] = jnp.dot(
+                hits, tok_all[k], preferred_element_type=F32
+            ).astype(BF16)
+
+        def one(p, carry):
+            whole_copy(p, 1, sem, expert_at(p)).start()
+            return carry
+
+        lax.fori_loop(first, last, one, 0)
+
+    dispatch_whole(far_blocks, near_blocks, experts - 1, 1)
     own_copy = pltpu.make_async_copy(
-        near_out.at[:, blocks(per_chunk - 1, 1), :],
+        near_out.at[:, blocks(experts - 1 - ring_blocks, 1), :],
         exp_all.at[:, blocks(experts - 1, 1), :],
         local_sem.at[5],
     )
     own_copy.start()
+    dispatch_whole(ring_blocks, mid_blocks, far_blocks, 2)
 
     def all_near():
-        return remote(
-            near_out.at[:, blocks(0, per_chunk - 1), :],
-            exp_all.at[:, blocks(far_blocks, per_chunk - 1), :],
-            dis_ss.at[1], dis_rs.at[1], "expert", lax.rem(mine + 1, experts),
-        )
+        return whole_copy(far_blocks, near_blocks - 1, 1, anyone)
+
+    def all_mid():
+        return whole_copy(ring_blocks, mid_blocks, 2, anyone)
 
     gain = gain_row[...]
     weight_copies[0].wait()
@@ -264,10 +282,9 @@
     own_back.start()
 
     def all_near_back():
-        others = blocks(0, per_chunk - 1)
+        others = blocks(0, near_blocks - 1)
         return remote(
-            near_ret.at[others], near_in.at[others], ret_ss.at[1], ret_rs.at[1], "expert",
-            lax.rem(mine + 1, experts),
+            near_ret.at[others], near_in.at[others], ret_ss.at[1], ret_rs.at[1], "expert", anyone,
         )
 
     for j in range(done, messages):
@@ -308,42 +325,21 @@
     res_sums = (res_part, rs_send, rs_recv, rs_ss, rs_rs)
     exp_sums = (exp_part, es_send, es_recv, es_ss, es_rs)
 
-    def expert(c, carry):
+    def expert(c):
         rows, part = expert_rows(c)
         for k in range(ring):
             exp_part[k, rows, :] = part[:, k * width : (k + 1) * width]
-        scatter_send(exp_sums, c, 0)
-        scatter_send(exp_sums, c, 1)
-        return carry
-
-    lax.fori_loop(0, chunks - 1, expert, 0)
-
-    def wave(j):
-        def one(c, carry):
-            scatter_send(exp_sums, c, j)
-            return carry
-
-        lax.fori_loop(0, chunks - 1, one, 0)
-
-    wave(2)
-
-    own_back.wait()
-    all_near_back().wait_recv()
-    near_rows = pl.ds(far_rows, chunk_rows)
-    for tile in range(tiles):
-        rows = pl.ds(tile * res_rows, res_rows)
-        back = jnp.dot(table[rows, near_rows], near_in[...], preferred_element_type=F32)
-        gates = gate_cols[rows, :]
-        for k in range(ring):
-            res_part[k, rows, :] += gates * back[:, k * width : (k + 1) * width]
-    scatter_send(res_sums, 0, 0)
-    scatter_send(res_sums, 0, 1)
-
-    for j in range(3, messages):
-        wave(j)
-    early = min(4, messages)
-    for j in range(2, early):
-        scatter_send(res_sums, 0, j)
+
+    def merge():
+        own_back.wait()
+        all_near_back().wait_recv()
+        near_rows = pl.ds(far_rows, chunk_rows)
+        for tile in range(tiles):
+            rows = pl.ds(tile * res_rows, res_rows)
+            back = jnp.dot(table[rows, near_rows], near_in[...], preferred_element_type=F32)
+            gates = gate_cols[rows, :]
+            for k in range(ring):
+                res_part[k, rows, :] += gates * back[:, k * width : (k + 1) * width]
 
     def give_back(p, carry):
         remote(
@@ -353,32 +349,67 @@
         return carry
 
     half_rows = chunk_rows // 2
-    for c in range(chunks - 1):
+
+    def finish(c):
         for h in (0, 1):
             ret_send[pl.ds(c * chunk_rows + h * half_rows, half_rows), :] = scatter_sum(
                 exp_sums, c, h
             ).astype(BF16)
         lax.fori_loop(c * per_chunk, (c + 1) * per_chunk, give_back, 0)
 
-    for j in range(early, messages):
-        scatter_send(res_sums, 0, j)
+    def term(c, *steps):
+        for j in steps:
+            if j < messages:
+                scatter_send(exp_sums, c, j)
+
+    def res_term(*steps):
+        for j in steps:
+            if j < messages:
+                scatter_send(res_sums, 0, j)
+
+    expert(0)
+    term(0, 0, 1)
+    expert(1)
+    term(1, 0, 1)
+    all_mid().wait_recv()
+    expert(2)
+    term(0, 2, 3)
+    term(2, 0, 1)
+    term(0, 4, 5)
+    term(1, 2, 3)
+    term(0, 6)
+    term(2, 2, 3)
+    merge()
+    term(1, 4, 5)
+    finish(0)
+    res_term(0)
+    term(2, 4, 5)
+    term(1, 6)
+    term(2, 6)
+    res_term(1)
+    finish(1)
+    finish(2)
+    res_term(2, 3, 4, 5, 6)
 
     def all_returned():
         return remote(
-            ret_send.at[far], returned.at[far], ret_ss.at[0], ret_rs.at[0], "expert",
-            lax.rem(mine + 1, experts),
+            ret_send.at[far], returned.at[far], ret_ss.at[0], ret_rs.at[0], "expert", anyone,
         )
 
     all_returned().wait_recv()
     half = tokens // 2
-    for h in (1, 0):
-        rows = pl.ds(h * half, half)
-        moe = jnp.dot(table[rows, pl.ds(0, far_rows)], returned[...], preferred_element_type=F32)
-        gated = gate_cols[rows, :] * moe
-        out[rows, :] = (scatter_sum(res_sums, 0, h) + gated).astype(BF16)
+    halves = [pl.ds(h * half, half) for h in (0, 1)]
+    gated = [
+        gate_cols[rows, :]
+        * jnp.dot(table[rows, pl.ds(0, far_rows)], returned[...], preferred_element_type=F32)
+        for rows in halves
+    ]
+    for h, rows in enumerate(halves):
+        out[rows, :] = scatter_sum(res_sums, 0, h) + gated[h]
 
     all_dispatched().wait_send()
     all_near().wait_send()
+    all_mid().wait_send()
     all_near_back().wait_send()
     all_returned().wait_send()
     for j in range(messages):
@@ -409,6 +440,7 @@
     messages = ring - 1
     near_rows = total // chunks
     far_rows = total - near_rows
+    ring_rows = far_rows - near_rows // 2
 
     any_space = pl.BlockSpec(memory_space=pl.ANY)
     in_vmem = pl.BlockSpec(memory_space=pltpu.VMEM)
@@ -416,7 +448,7 @@
     res_half, exp_half = count // 2, total // chunks // 2
     return pl.pallas_call(
         functools.partial(layer_kernel, experts, ring, slots, chunks),
-        out_shape=jax.ShapeDtypeStruct((count, width), BF16),
+        out_shape=jax.ShapeDtypeStruct((count, width), F32),
         in_specs=[any_space] * 9,
         out_specs=in_vmem,
         scratch_shapes=[
@@ -426,8 +458,8 @@
             pltpu.VMEM((1, model), F32),
             pltpu.VMEM((ring, count, width), BF16),
             pltpu.VMEM((ring, total, width), BF16),
-            pltpu.VMEM((far_rows, width), BF16),
-            pltpu.VMEM((ring, near_rows, width), BF16),
+            pltpu.VMEM((ring_rows, width), BF16),
+            pltpu.VMEM((ring, total - ring_rows, width), BF16),
             pltpu.VMEM((model, hidden), BF16),
             pltpu.VMEM((hidden, model), BF16),
             pltpu.VMEM((model, hidden), BF16),
@@ -449,8 +481,8 @@
             sems((2, messages)),
             sems((2, messages)),
             sems((2, messages)),
-            sems((2,)),
-            sems((2,)),
+            sems((3,)),
+            sems((3,)),
             sems((2, 1, messages)),
             sems((2, 1, messages)),
             sems((2, chunks - 1, messages)),
@@ -465,7 +497,7 @@
     )(
         expert_of.reshape(-1, width), slot_of.reshape(-1, width), gate_prob.reshape(-1, width),
         gain.reshape(1, model), tokens, w_res_in, w_res_out, w_exp_in[0], w_exp_out[0],
-    )
+    ).astype(BF16)
 
 
 def solution(mesh):

time: 122 us -> 121 us (level); the launches traced: 121 us -> 121 us
  other arithmetic: 0 us -> 1.69 us
  local copies, waits for them, and re-layouts: 1.62 us -> 0 us
    convert_element_type x0 -> x1, other arithmetic: none -> 1.69 us  [per_device(): return pl.pallas_call(functools.partial(layer_kernel, experts, ring, slot...]
    unnamed x1 -> x0, local copies, waits for them, and re-layouts: 1.62 us -> none
where the time goes in v3:
time: 121 us
  Pallas kernels  120 us (99%)
  other arithmetic  1.69 us (1%)
    pallas_call x1, Pallas kernels, per_device(): pl.pallas_call(functools.partial(layer_kernel, experts, ring, slots, chun...  120 us

profile of v3, /device:TPU:80, one launch (start us, length us, event | category | flops | bytes accessed | tf_op | source)
XLA Modules:
  0.0 121.3 jit_solution(1065756383496476221)
XLA Ops:
  0.0 119.6 %moe_layer.1 = f32[768,128]{1,0:T(8,128)} custom-call(s32[6,128]{1,0:T(8,128)} %bitcast.8, s32[6,128]{1,0:T(8,128)} %bitcast.9, f32[6,128]{1,0:T(8,128)} %bitcast.10, f32[1,1024]{1,0:T(1,128)} %bitcast.11, bf16[768,128]{1,0:T(8,128)(2,1)} %tok_hbm.1, bf16[1024,512]{1,0:T(8,128)(2,1)} %wri_hbm.1, bf16[512,1024]{1,0:T(8,128)(2,1)} %wro_hbm.1, ...), custom_call_target="tpu_custom_call" | custom-call | tf_op jit(solution)/shard_map/moe_layer/pallas_call | solution.py:449
  119.6 1.7 %convert_element_type.3 = bf16[768,128]{1,0:T(8,128)(2,1)} convert(f32[768,128]{1,0:T(8,128)} %moe_layer.1) | non-fusion elementwise | flops 98304 | bytes 589824 | tf_op jit(solution)/shard_map/convert_element_type | solution.py:500

commit v4 on v3

--- a/solution.py
+++ b/solution.py
@@ -35,7 +35,7 @@
 
 
 def layer_kernel(
-    experts, ring, slots, chunks,
+    experts, ring, slots, chunks, tiles, pieces,
     ids_hbm, slots_hbm, gate_hbm, gain_hbm, tok_hbm, wri_hbm, wro_hbm, wei_hbm, weo_hbm, out,
     ids, slot, gate, gain_row, tok_all, exp_all, outgoing, near_out, wri, wro, wei, weo,
     res_part, exp_part, rs_send, rs_recv, es_send, es_recv, ret_send, returned,
@@ -117,28 +117,31 @@
     tok_copy.wait()
     pl.semaphore_wait(barrier, experts + 1)
 
+    gathered = messages * pieces // 2
+
     def gather_copy(refs, j, way, arriving):
         buf, rows, send_sem, recv_sem = refs
         turn = 1 - 2 * way
-        half = rows // 2
-        shard = on_ring(-turn * (j // 2 + (1 if arriving else 0)))
-        ref = buf.at[shard, pl.ds(((j + way) % 2) * half, half)]
+        size = rows // pieces
+        shard = on_ring(-turn * (j // pieces + (1 if arriving else 0)))
+        piece = (j + way * (pieces // 2)) % pieces
+        ref = buf.at[shard, pl.ds(piece * size, size)]
         return remote(ref, ref, send_sem.at[way, j], recv_sem.at[way, j], "mp", on_ring(turn))
 
-    def gather_send(refs, j):
-        for way in (0, 1):
-            gather_copy(refs, j, way, False).start()
+    def gather_send(refs):
+        for j in range(pieces):
+            for way in (0, 1):
+                gather_copy(refs, j, way, False).start()
 
     def gather_step(refs, j):
         for way in (0, 1):
             gather_copy(refs, j, way, True).wait_recv()
-            if j + 2 < messages:
-                gather_copy(refs, j + 2, way, False).start()
+            if j + pieces < gathered:
+                gather_copy(refs, j + pieces, way, False).start()
 
     tok_ring = (tok_all, tokens, tok_ss, tok_rs)
     exp_ring = (exp_all, ring_rows, exp_ss, exp_rs)
-    gather_send(tok_ring, 0)
-    gather_send(tok_ring, 1)
+    gather_send(tok_ring)
 
     def as_row(values):
         return jnp.concatenate([values[at : at + 1] for at in range(values.shape[0])], axis=1)
@@ -187,7 +190,7 @@
         hit = jnp.where(slot_cols[:, :wide] == wanted[:, at : at + wide], 1.0, 0.0)
         table[:, at : at + wide] = hit.astype(BF16)
 
-    for j in range(messages - 2):
+    for j in range(gathered - pieces):
         gather_step(tok_ring, j)
 
     anyone = lax.rem(mine + 1, experts)
@@ -200,9 +203,8 @@
         )
 
     all_dispatched().wait_recv()
-    gather_send(exp_ring, 0)
-    gather_send(exp_ring, 1)
-    for j in range(messages - 2, messages):
+    gather_send(exp_ring)
+    for j in range(gathered - pieces, gathered):
         gather_step(tok_ring, j)
 
     def whole_copy(first, count, sem, target):
@@ -233,6 +235,13 @@
         local_sem.at[5],
     )
     own_copy.start()
+    exp_steps = iter(range(gathered))
+
+    def exp_advance(count):
+        for j in range(count):
+            gather_step(exp_ring, next(exp_steps))
+
+    exp_advance(1)
     dispatch_whole(ring_blocks, mid_blocks, far_blocks, 2)
 
     def all_near():
@@ -244,17 +253,16 @@
     gain = gain_row[...]
     weight_copies[0].wait()
     weight_copies[1].wait()
-    tiles = 3 if tokens % 48 == 0 else 1
     res_rows = tokens // tiles
+    relayed = gathered - pieces
     for tile in range(tiles):
+        exp_advance((relayed - 1) // (tiles + 1))
         rows = pl.ds(tile * res_rows, res_rows)
         normed = rms_rows([tok_all[k, rows, :] for k in range(ring)], gain)
         part = mlp_rows(normed, wri, wro)
         for k in range(ring):
             res_part[k, rows, :] = part[:, k * width : (k + 1) * width]
-        if tile < messages - 3:
-            gather_step(exp_ring, tile)
-    done = min(tiles, messages - 3)
+    exp_advance(relayed - 1 - tiles * ((relayed - 1) // (tiles + 1)))
 
     def expert_rows(c):
         rows = pl.ds(pl.multiple_of(c * chunk_rows, chunk_rows), chunk_rows)
@@ -287,8 +295,7 @@
             near_ret.at[others], near_in.at[others], ret_ss.at[1], ret_rs.at[1], "expert", anyone,
         )
 
-    for j in range(done, messages):
-        gather_step(exp_ring, j)
+    exp_advance(pieces)
 
     def scatter_copy(refs, c, j, way):
         send, recv, send_sem, recv_sem = refs[1:]
@@ -357,39 +364,37 @@
             ).astype(BF16)
         lax.fori_loop(c * per_chunk, (c + 1) * per_chunk, give_back, 0)
 
-    def term(c, *steps):
+    def wave(refs, count, *steps):
+        def one(c, carry, j=0):
+            scatter_send(refs, c, j)
+            return carry
+
         for j in steps:
             if j < messages:
-                scatter_send(exp_sums, c, j)
-
-    def res_term(*steps):
-        for j in steps:
-            if j < messages:
-                scatter_send(res_sums, 0, j)
-
-    expert(0)
-    term(0, 0, 1)
-    expert(1)
-    term(1, 0, 1)
-    all_mid().wait_recv()
-    expert(2)
-    term(0, 2, 3)
-    term(2, 0, 1)
-    term(0, 4, 5)
-    term(1, 2, 3)
-    term(0, 6)
-    term(2, 2, 3)
+                lax.fori_loop(0, count, functools.partial(one, j=j), 0)
+
+    def exp_wave(*steps):
+        wave(exp_sums, chunks - 1, *steps)
+
+    def res_wave(*steps):
+        wave(res_sums, tiles, *steps)
+
+    for c in range(chunks - 1):
+        if c == chunks - 2:
+            all_mid().wait_recv()
+        expert(c)
+        scatter_send(exp_sums, c, 0)
+        scatter_send(exp_sums, c, 1)
+    exp_wave(2)
     merge()
-    term(1, 4, 5)
-    finish(0)
-    res_term(0)
-    term(2, 4, 5)
-    term(1, 6)
-    term(2, 6)
-    res_term(1)
-    finish(1)
-    finish(2)
-    res_term(2, 3, 4, 5, 6)
+    res_wave(0)
+    exp_wave(3, 4)
+    res_wave(1)
+    exp_wave(5, 6)
+    res_wave(2)
+    for c in range(chunks - 1):
+        finish(c)
+    res_wave(3, 4, 5, 6)
 
     def all_returned():
         return remote(
@@ -397,34 +402,34 @@
         )
 
     all_returned().wait_recv()
-    half = tokens // 2
-    halves = [pl.ds(h * half, half) for h in (0, 1)]
+    half = res_rows // 2
+    parts = [pl.ds(at * half, half) for at in range(2 * tiles)]
     gated = [
         gate_cols[rows, :]
         * jnp.dot(table[rows, pl.ds(0, far_rows)], returned[...], preferred_element_type=F32)
-        for rows in halves
+        for rows in parts
     ]
-    for h, rows in enumerate(halves):
-        out[rows, :] = scatter_sum(res_sums, 0, h) + gated[h]
+    for at, rows in enumerate(parts):
+        out[rows, :] = scatter_sum(res_sums, at // 2, at % 2) + gated[at]
 
     all_dispatched().wait_send()
     all_near().wait_send()
     all_mid().wait_send()
     all_near_back().wait_send()
     all_returned().wait_send()
-    for j in range(messages):
+    for j in range(gathered):
         for way in (0, 1):
             gather_copy(tok_ring, j, way, False).wait_send()
             gather_copy(exp_ring, j, way, False).wait_send()
-            scatter_copy(res_sums, 0, j, way).wait_send()
-
-    def drain(c, carry):
+
+    def drain(refs, c, carry):
         for j in range(messages):
             for way in (0, 1):
-                scatter_copy(exp_sums, c, j, way).wait_send()
+                scatter_copy(refs, c, j, way).wait_send()
         return carry
 
-    lax.fori_loop(0, chunks - 1, drain, 0)
+    lax.fori_loop(0, tiles, functools.partial(drain, res_sums), 0)
+    lax.fori_loop(0, chunks - 1, functools.partial(drain, exp_sums), 0)
 
 
 def per_device(
@@ -445,9 +450,12 @@
     any_space = pl.BlockSpec(memory_space=pl.ANY)
     in_vmem = pl.BlockSpec(memory_space=pltpu.VMEM)
     sems = pltpu.SemaphoreType.DMA
-    res_half, exp_half = count // 2, total // chunks // 2
+    tiles = 3 if count % 96 == 0 else 1
+    pieces = 4
+    gathered = messages * pieces // 2
+    res_half, exp_half = count // tiles // 2, total // chunks // 2
     return pl.pallas_call(
-        functools.partial(layer_kernel, experts, ring, slots, chunks),
+        functools.partial(layer_kernel, experts, ring, slots, chunks, tiles, pieces),
         out_shape=jax.ShapeDtypeStruct((count, width), F32),
         in_specs=[any_space] * 9,
         out_specs=in_vmem,
@@ -466,8 +474,8 @@
             pltpu.VMEM((hidden, model), BF16),
             pltpu.VMEM((ring, count, width), F32),
             pltpu.VMEM((ring, far_rows, width), F32),
-            pltpu.VMEM((2, 1, messages, res_half, width), BF16),
-            pltpu.VMEM((2, 1, messages, res_half, width), BF16),
+            pltpu.VMEM((2, tiles, messages, res_half, width), BF16),
+            pltpu.VMEM((2, tiles, messages, res_half, width), BF16),
             pltpu.VMEM((2, chunks - 1, messages, exp_half, width), BF16),
             pltpu.VMEM((2, chunks - 1, messages, exp_half, width), BF16),
             pltpu.VMEM((far_rows, width), BF16),
@@ -477,14 +485,14 @@
             pltpu.VMEM((count, total), BF16),
             pltpu.VMEM((count, width), F32),
             sems((11,)),
-            sems((2, messages)),
-            sems((2, messages)),
-            sems((2, messages)),
-            sems((2, messages)),
+            sems((2, gathered)),
+            sems((2, gathered)),
+            sems((2, gathered)),
+            sems((2, gathered)),
             sems((3,)),
             sems((3,)),
-            sems((2, 1, messages)),
-            sems((2, 1, messages)),
+            sems((2, tiles, messages)),
+            sems((2, tiles, messages)),
             sems((2, chunks - 1, messages)),
             sems((2, chunks - 1, messages)),
             sems((2,)),

time: 121 us -> 120 us (level)
  Pallas kernels: 120 us -> 118 us
    pallas_call x1, Pallas kernels: 120 us -> 118 us  [per_device(): pl.pallas_call(functools.partial(layer_kernel, experts, ring, slots, chun...]
where the time goes in v4:
time: 120 us
  Pallas kernels  118 us (98%)
  other arithmetic  1.69 us (1%)
    pallas_call x1, Pallas kernels, per_device(): pl.pallas_call(functools.partial(layer_kernel, experts, ring, slots, chun...  118 us

profile of v4, /device:TPU:80, one launch (start us, length us, event | category | flops | bytes accessed | tf_op | source)
XLA Modules:
  0.0 120.0 jit_solution(110436557456666859)
XLA Ops:
  0.0 118.3 %moe_layer.1 = f32[768,128]{1,0:T(8,128)} custom-call(s32[6,128]{1,0:T(8,128)} %bitcast.8, s32[6,128]{1,0:T(8,128)} %bitcast.9, f32[6,128]{1,0:T(8,128)} %bitcast.10, f32[1,1024]{1,0:T(1,128)} %bitcast.11, bf16[768,128]{1,0:T(8,128)(2,1)} %tok_hbm.1, bf16[1024,512]{1,0:T(8,128)(2,1)} %wri_hbm.1, bf16[512,1024]{1,0:T(8,128)(2,1)} %wro_hbm.1, ...), custom_call_target="tpu_custom_call" | custom-call | tf_op jit(solution)/shard_map/moe_layer/pallas_call | solution.py:457
  118.3 1.7 %convert_element_type.3 = bf16[768,128]{1,0:T(8,128)(2,1)} convert(f32[768,128]{1,0:T(8,128)} %moe_layer.1) | non-fusion elementwise | flops 98304 | bytes 589824 | tf_op jit(solution)/shard_map/convert_element_type | solution.py:508

commit v5 on v4

--- a/solution.py
+++ b/solution.py
@@ -39,8 +39,8 @@
     ids_hbm, slots_hbm, gate_hbm, gain_hbm, tok_hbm, wri_hbm, wro_hbm, wei_hbm, weo_hbm, out,
     ids, slot, gate, gain_row, tok_all, exp_all, outgoing, near_out, wri, wro, wei, weo,
     res_part, exp_part, rs_send, rs_recv, es_send, es_recv, ret_send, returned,
-    near_ret, near_in, table, gate_cols,
-    local_sem, tok_ss, tok_rs, exp_ss, exp_rs, dis_ss, dis_rs,
+    near_ret, near_in, table, gate_cols, result,
+    local_sem, out_sem, tok_ss, tok_rs, exp_ss, exp_rs, dis_ss, dis_rs,
     rs_ss, rs_rs, es_ss, es_rs, ret_ss, ret_rs,
 ):
     me = lax.axis_index("mp")
@@ -364,37 +364,52 @@
             ).astype(BF16)
         lax.fori_loop(c * per_chunk, (c + 1) * per_chunk, give_back, 0)
 
-    def wave(refs, count, *steps):
+    def wave(refs, first, last, *steps):
         def one(c, carry, j=0):
             scatter_send(refs, c, j)
             return carry
 
         for j in steps:
             if j < messages:
-                lax.fori_loop(0, count, functools.partial(one, j=j), 0)
-
-    def exp_wave(*steps):
-        wave(exp_sums, chunks - 1, *steps)
+                lax.fori_loop(first, last, functools.partial(one, j=j), 0)
+
+    lead = chunks - 2
+
+    def lead_wave(*steps):
+        wave(exp_sums, 0, lead, *steps)
+
+    def last_wave(*steps):
+        wave(exp_sums, lead, lead + 1, *steps)
 
     def res_wave(*steps):
-        wave(res_sums, tiles, *steps)
-
-    for c in range(chunks - 1):
-        if c == chunks - 2:
-            all_mid().wait_recv()
+        wave(res_sums, 0, tiles, *steps)
+
+    for c in range(lead):
         expert(c)
         scatter_send(exp_sums, c, 0)
         scatter_send(exp_sums, c, 1)
-    exp_wave(2)
+    lead_wave(2)
+    all_mid().wait_recv()
+    expert(lead)
+    last_wave(0, 1)
+    lead_wave(3, 4)
+    last_wave(2)
     merge()
     res_wave(0)
-    exp_wave(3, 4)
+    lead_wave(5)
+    last_wave(3)
+    lead_wave(6)
+    last_wave(4)
     res_wave(1)
-    exp_wave(5, 6)
+    for c in range(lead):
+        finish(c)
     res_wave(2)
-    for c in range(chunks - 1):
-        finish(c)
-    res_wave(3, 4, 5, 6)
+    last_wave(5)
+    res_wave(3)
+    last_wave(6)
+    res_wave(4)
+    finish(lead)
+    res_wave(5, 6)
 
     def all_returned():
         return remote(
@@ -409,8 +424,12 @@
         * jnp.dot(table[rows, pl.ds(0, far_rows)], returned[...], preferred_element_type=F32)
         for rows in parts
     ]
+    writes = []
     for at, rows in enumerate(parts):
-        out[rows, :] = scatter_sum(res_sums, at // 2, at % 2) + gated[at]
+        value = scatter_sum(res_sums, at // 2, at % 2) + gated[at]
+        result[rows, :] = value.astype(BF16)
+        writes.append(pltpu.make_async_copy(result.at[rows], out.at[rows], out_sem.at[at]))
+        writes[at].start()
 
     all_dispatched().wait_send()
     all_near().wait_send()
@@ -430,6 +449,8 @@
 
     lax.fori_loop(0, tiles, functools.partial(drain, res_sums), 0)
     lax.fori_loop(0, chunks - 1, functools.partial(drain, exp_sums), 0)
+    for write in writes:
+        write.wait()
 
 
 def per_device(
@@ -448,7 +469,6 @@
     ring_rows = far_rows - near_rows // 2
 
     any_space = pl.BlockSpec(memory_space=pl.ANY)
-    in_vmem = pl.BlockSpec(memory_space=pltpu.VMEM)
     sems = pltpu.SemaphoreType.DMA
     tiles = 3 if count % 96 == 0 else 1
     pieces = 4
@@ -456,9 +476,9 @@
     res_half, exp_half = count // tiles // 2, total // chunks // 2
     return pl.pallas_call(
         functools.partial(layer_kernel, experts, ring, slots, chunks, tiles, pieces),
-        out_shape=jax.ShapeDtypeStruct((count, width), F32),
+        out_shape=jax.ShapeDtypeStruct((count, width), BF16),
         in_specs=[any_space] * 9,
-        out_specs=in_vmem,
+        out_specs=any_space,
         scratch_shapes=[
             pltpu.VMEM((count // width, width), jnp.int32),
             pltpu.VMEM((count // width, width), jnp.int32),
@@ -484,7 +504,9 @@
             pltpu.VMEM((near_rows, model), BF16),
             pltpu.VMEM((count, total), BF16),
             pltpu.VMEM((count, width), F32),
+            pltpu.VMEM((count, width), BF16),
             sems((11,)),
+            sems((2 * tiles,)),
             sems((2, gathered)),
             sems((2, gathered)),
             sems((2, gathered)),
@@ -505,7 +527,7 @@
     )(
         expert_of.reshape(-1, width), slot_of.reshape(-1, width), gate_prob.reshape(-1, width),
         gain.reshape(1, model), tokens, w_res_in, w_res_out, w_exp_in[0], w_exp_out[0],
-    ).astype(BF16)
+    )
 
 
 def solution(mesh):

time: 120 us -> 117 us (0.975)
  Pallas kernels: 118 us -> 115 us
  other arithmetic: 1.69 us -> 0 us
  local copies, waits for them, and re-layouts: 0 us -> 1.62 us
    pallas_call x1, Pallas kernels: 118 us -> 115 us  [per_device(): pl.pallas_call(functools.partial(layer_kernel, experts, ring, slots, chun...]
    convert_element_type x1 -> x0, other arithmetic: 1.69 us -> none  [per_device(): return pl.pallas_call(functools.partial(layer_kernel, experts, ring, slot...]
    unnamed x0 -> x1, local copies, waits for them, and re-layouts: none -> 1.62 us
where the time goes in v5:
time: 117 us; the launch traced here: 116 us
  Pallas kernels  115 us (98%)
  local copies, waits for them, and re-layouts  1.62 us (1%)
    pallas_call x1, Pallas kernels, per_device(): pl.pallas_call(functools.partial(layer_kernel, experts, ring, slots, chun...  115 us

profile of v5, /device:TPU:80, one launch (start us, length us, event | category | flops | bytes accessed | tf_op | source)
XLA Modules:
  0.0 116.3 jit_solution(4223582654915699375)
XLA Ops:
  0.0 114.7 %moe_layer.1 = bf16[768,128]{1,0:T(8,128)(2,1)} custom-call(s32[6,128]{1,0:T(8,128)} %bitcast.8, s32[6,128]{1,0:T(8,128)} %bitcast.9, f32[6,128]{1,0:T(8,128)} %bitcast.10, f32[1,1024]{1,0:T(1,128)} %bitcast.11, bf16[768,128]{1,0:T(8,128)(2,1)} %tok_hbm.1, bf16[1024,512]{1,0:T(8,128)(2,1)} %wri_hbm.1, bf16[512,1024]{1,0:T(8,128)(2,1)} %wro_hbm.1, ...), custom_call_target="tpu_custom_call" | custom-call | tf_op jit(solution)/shard_map/moe_layer/pallas_call | solution.py:477
  114.7 1.6 %copy.11 = bf16[768,128]{1,0:T(8,128)(2,1)} copy(bf16[768,128]{1,0:T(8,128)(2,1)} %moe_layer.1) | data formatting | bytes 393216

commit v6 on v5

--- a/solution.py
+++ b/solution.py
@@ -39,8 +39,8 @@
     ids_hbm, slots_hbm, gate_hbm, gain_hbm, tok_hbm, wri_hbm, wro_hbm, wei_hbm, weo_hbm, out,
     ids, slot, gate, gain_row, tok_all, exp_all, outgoing, near_out, wri, wro, wei, weo,
     res_part, exp_part, rs_send, rs_recv, es_send, es_recv, ret_send, returned,
-    near_ret, near_in, table, gate_cols, result,
-    local_sem, out_sem, tok_ss, tok_rs, exp_ss, exp_rs, dis_ss, dis_rs,
+    near_ret, near_in, table, gate_cols,
+    local_sem, tok_ss, tok_rs, exp_ss, exp_rs, dis_ss, dis_rs,
     rs_ss, rs_rs, es_ss, es_rs, ret_ss, ret_rs,
 ):
     me = lax.axis_index("mp")
@@ -51,7 +51,7 @@
     chunk_rows = total // chunks
     per_chunk = experts // chunks
     near_blocks = per_chunk
-    mid_blocks = per_chunk // 2
+    mid_blocks = per_chunk // 4 or 1
     far_blocks = experts - near_blocks
     ring_blocks = far_blocks - mid_blocks
     far_rows = far_blocks * slots
@@ -163,7 +163,7 @@
         ).start()
         return carry
 
-    group = mid_blocks
+    group = ring_blocks // 2 if ring_blocks % 2 == 0 else ring_blocks
 
     def pick(c, carry):
         rows = pl.ds(pl.multiple_of(c * group * slots, slots), group * slots)
@@ -388,28 +388,28 @@
         expert(c)
         scatter_send(exp_sums, c, 0)
         scatter_send(exp_sums, c, 1)
-    lead_wave(2)
     all_mid().wait_recv()
     expert(lead)
     last_wave(0, 1)
-    lead_wave(3, 4)
+    lead_wave(2)
     last_wave(2)
+    lead_wave(3)
     merge()
     res_wave(0)
+    lead_wave(4)
+    last_wave(3)
     lead_wave(5)
-    last_wave(3)
+    res_wave(1)
     lead_wave(6)
     last_wave(4)
-    res_wave(1)
     for c in range(lead):
         finish(c)
+    last_wave(5)
     res_wave(2)
-    last_wave(5)
+    last_wave(6)
     res_wave(3)
-    last_wave(6)
-    res_wave(4)
     finish(lead)
-    res_wave(5, 6)
+    res_wave(4, 5, 6)
 
     def all_returned():
         return remote(
@@ -424,12 +424,9 @@
         * jnp.dot(table[rows, pl.ds(0, far_rows)], returned[...], preferred_element_type=F32)
         for rows in parts
     ]
-    writes = []
     for at, rows in enumerate(parts):
         value = scatter_sum(res_sums, at // 2, at % 2) + gated[at]
-        result[rows, :] = value.astype(BF16)
-        writes.append(pltpu.make_async_copy(result.at[rows], out.at[rows], out_sem.at[at]))
-        writes[at].start()
+        out[rows, :] = value.astype(BF16)
 
     all_dispatched().wait_send()
     all_near().wait_send()
@@ -449,8 +446,6 @@
 
     lax.fori_loop(0, tiles, functools.partial(drain, res_sums), 0)
     lax.fori_loop(0, chunks - 1, functools.partial(drain, exp_sums), 0)
-    for write in writes:
-        write.wait()
 
 
 def per_device(
@@ -466,7 +461,7 @@
     messages = ring - 1
     near_rows = total // chunks
     far_rows = total - near_rows
-    ring_rows = far_rows - near_rows // 2
+    ring_rows = far_rows - (experts // chunks // 4 or 1) * slots
 
     any_space = pl.BlockSpec(memory_space=pl.ANY)
     sems = pltpu.SemaphoreType.DMA
@@ -476,9 +471,9 @@
     res_half, exp_half = count // tiles // 2, total // chunks // 2
     return pl.pallas_call(
         functools.partial(layer_kernel, experts, ring, slots, chunks, tiles, pieces),
-        out_shape=jax.ShapeDtypeStruct((count, width), BF16),
+        out_shape=pltpu.VMEM((count, width), BF16),
         in_specs=[any_space] * 9,
-        out_specs=any_space,
+        out_specs=pl.BlockSpec(memory_space=pltpu.VMEM),
         scratch_shapes=[
             pltpu.VMEM((count // width, width), jnp.int32),
             pltpu.VMEM((count // width, width), jnp.int32),
@@ -504,9 +499,7 @@
             pltpu.VMEM((near_rows, model), BF16),
             pltpu.VMEM((count, total), BF16),
             pltpu.VMEM((count, width), F32),
-            pltpu.VMEM((count, width), BF16),
             sems((11,)),
-            sems((2 * tiles,)),
             sems((2, gathered)),
             sems((2, gathered)),
             sems((2, gathered)),

time: 117 us -> 115 us (0.983)
    pallas_call x1, Pallas kernels: 115 us -> 114 us  [per_device(): pl.pallas_call(functools.partial(layer_kernel, experts, ring, slots, chun...]
where the time goes in v6:
time: 115 us; the launch traced here: 114 us
  Pallas kernels  114 us (99%)
    pallas_call x1, Pallas kernels, per_device(): pl.pallas_call(functools.partial(layer_kernel, experts, ring, slots, chun...  114 us

profile of v6, /device:TPU:80, one launch (start us, length us, event | category | flops | bytes accessed | tf_op | source)
XLA Modules:
  0.0 114.2 jit_solution(1346311203980089868)
XLA Ops:
  0.0 113.5 %moe_layer.1 = bf16[768,128]{1,0:T(8,128)(2,1)S(1)} custom-call(s32[6,128]{1,0:T(8,128)} %bitcast.8, s32[6,128]{1,0:T(8,128)} %bitcast.9, f32[6,128]{1,0:T(8,128)} %bitcast.10, f32[1,1024]{1,0:T(1,128)} %bitcast.11, bf16[768,128]{1,0:T(8,128)(2,1)} %tok_hbm.1, bf16[1024,512]{1,0:T(8,128)(2,1)} %wri_hbm.1, bf16[512,1024]{1,0:T(8,128)(2,1)} %wro_hbm.1, ...), custom_call_target="tpu_custom_call" | custom-call | tf_op jit(solution)/shard_map/moe_layer/pallas_call | solution.py:472
  113.5 0.7 copy.11

commit v7 on v6

--- a/solution.py
+++ b/solution.py
@@ -35,7 +35,7 @@
 
 
 def layer_kernel(
-    experts, ring, slots, chunks, tiles, pieces,
+    experts, ring, slots, chunks, tiles, tok_pieces, pieces,
     ids_hbm, slots_hbm, gate_hbm, gain_hbm, tok_hbm, wri_hbm, wro_hbm, wei_hbm, weo_hbm, out,
     ids, slot, gate, gain_row, tok_all, exp_all, outgoing, near_out, wri, wro, wei, weo,
     res_part, exp_part, rs_send, rs_recv, es_send, es_recv, ret_send, returned,
@@ -112,15 +112,11 @@
     ]
     for copy in weight_copies:
         copy.start()
-    for copy in small_copies:
-        copy.wait()
     tok_copy.wait()
     pl.semaphore_wait(barrier, experts + 1)
 
-    gathered = messages * pieces // 2
-
     def gather_copy(refs, j, way, arriving):
-        buf, rows, send_sem, recv_sem = refs
+        buf, rows, pieces, send_sem, recv_sem = refs
         turn = 1 - 2 * way
         size = rows // pieces
         shard = on_ring(-turn * (j // pieces + (1 if arriving else 0)))
@@ -129,19 +125,23 @@
         return remote(ref, ref, send_sem.at[way, j], recv_sem.at[way, j], "mp", on_ring(turn))
 
     def gather_send(refs):
-        for j in range(pieces):
+        for j in range(refs[2]):
             for way in (0, 1):
                 gather_copy(refs, j, way, False).start()
 
     def gather_step(refs, j):
         for way in (0, 1):
             gather_copy(refs, j, way, True).wait_recv()
-            if j + pieces < gathered:
-                gather_copy(refs, j + pieces, way, False).start()
-
-    tok_ring = (tok_all, tokens, tok_ss, tok_rs)
-    exp_ring = (exp_all, ring_rows, exp_ss, exp_rs)
+            if j + refs[2] < messages * refs[2] // 2:
+                gather_copy(refs, j + refs[2], way, False).start()
+
+    tok_ring = (tok_all, tokens, tok_pieces, tok_ss, tok_rs)
+    exp_ring = (exp_all, ring_rows, pieces, exp_ss, exp_rs)
+    tok_gathered = messages * tok_pieces // 2
+    gathered = messages * pieces // 2
     gather_send(tok_ring)
+    for copy in small_copies:
+        copy.wait()
 
     def as_row(values):
         return jnp.concatenate([values[at : at + 1] for at in range(values.shape[0])], axis=1)
@@ -190,7 +190,7 @@
         hit = jnp.where(slot_cols[:, :wide] == wanted[:, at : at + wide], 1.0, 0.0)
         table[:, at : at + wide] = hit.astype(BF16)
 
-    for j in range(gathered - pieces):
+    for j in range(tok_gathered - tok_pieces):
         gather_step(tok_ring, j)
 
     anyone = lax.rem(mine + 1, experts)
@@ -204,7 +204,7 @@
 
     all_dispatched().wait_recv()
     gather_send(exp_ring)
-    for j in range(gathered - pieces, gathered):
+    for j in range(tok_gathered - tok_pieces, tok_gathered):
         gather_step(tok_ring, j)
 
     def whole_copy(first, count, sem, target):
@@ -392,10 +392,10 @@
     expert(lead)
     last_wave(0, 1)
     lead_wave(2)
+    merge()
+    res_wave(0)
     last_wave(2)
     lead_wave(3)
-    merge()
-    res_wave(0)
     lead_wave(4)
     last_wave(3)
     lead_wave(5)
@@ -435,8 +435,10 @@
     all_returned().wait_send()
     for j in range(gathered):
         for way in (0, 1):
+            gather_copy(exp_ring, j, way, False).wait_send()
+    for j in range(tok_gathered):
+        for way in (0, 1):
             gather_copy(tok_ring, j, way, False).wait_send()
-            gather_copy(exp_ring, j, way, False).wait_send()
 
     def drain(refs, c, carry):
         for j in range(messages):
@@ -466,11 +468,11 @@
     any_space = pl.BlockSpec(memory_space=pl.ANY)
     sems = pltpu.SemaphoreType.DMA
     tiles = 3 if count % 96 == 0 else 1
-    pieces = 4
-    gathered = messages * pieces // 2
+    tok_pieces, pieces = 8, 4
+    tok_gathered, gathered = messages * tok_pieces // 2, messages * pieces // 2
     res_half, exp_half = count // tiles // 2, total // chunks // 2
     return pl.pallas_call(
-        functools.partial(layer_kernel, experts, ring, slots, chunks, tiles, pieces),
+        functools.partial(layer_kernel, experts, ring, slots, chunks, tiles, tok_pieces, pieces),
         out_shape=pltpu.VMEM((count, width), BF16),
         in_specs=[any_space] * 9,
         out_specs=pl.BlockSpec(memory_space=pltpu.VMEM),
@@ -500,8 +502,8 @@
             pltpu.VMEM((count, total), BF16),
             pltpu.VMEM((count, width), F32),
             sems((11,)),
-            sems((2, gathered)),
-            sems((2, gathered)),
+            sems((2, tok_gathered)),
+            sems((2, tok_gathered)),
             sems((2, gathered)),
             sems((2, gathered)),
             sems((3,)),

time: 115 us -> 117 us (1.017)
  Pallas kernels: 114 us -> 116 us
    pallas_call x1, Pallas kernels: 114 us -> 116 us  [per_device(): pl.pallas_call(functools.partial(layer_kernel, experts, ring, slots, chun...]
where the time goes in v7:
time: 117 us; the launch traced here: 116 us
  Pallas kernels  116 us (99%)
    pallas_call x1, Pallas kernels, per_device(): pl.pallas_call(functools.partial(layer_kernel, experts, ring, slots, chun...  116 us

profile of v7, /device:TPU:80, one launch (start us, length us, event | category | flops | bytes accessed | tf_op | source)
XLA Modules:
  0.0 116.3 jit_solution(4777497354623599234)
XLA Ops:
  0.0 115.6 %moe_layer.1 = bf16[768,128]{1,0:T(8,128)(2,1)S(1)} custom-call(s32[6,128]{1,0:T(8,128)} %bitcast.8, s32[6,128]{1,0:T(8,128)} %bitcast.9, f32[6,128]{1,0:T(8,128)} %bitcast.10, f32[1,1024]{1,0:T(1,128)} %bitcast.11, bf16[768,128]{1,0:T(8,128)(2,1)} %tok_hbm.1, bf16[1024,512]{1,0:T(8,128)(2,1)} %wri_hbm.1, bf16[512,1024]{1,0:T(8,128)(2,1)} %wro_hbm.1, ...), custom_call_target="tpu_custom_call" | custom-call | tf_op jit(solution)/shard_map/moe_layer/pallas_call | solution.py:474
  115.6 0.7 copy.11
